TPU v7x, 8 devices: a whole 2x2x1 slice. The times are simulated.
8 devices in a mesh: data: 2 (over z, y), tp: 4 (over x, core).
Axes of the slice: x: 2, y: 2, z: 1, core: 2. Of those that a mesh axis runs over, the one named last changes fastest.
Arguments:
- attn_out: bfloat16 [512, 8192], P('data', 'tp'), parts along dimension 0
- w_out: bfloat16 [8192, 8192], P('tp')
- residual: bfloat16 [512, 8192], P('data', 'tp'), parts along dimension 0
- norm_gain: float32 [8192], P('tp')
Outputs:
- output 1: bfloat16 [512, 8192], P('data', 'tp'), parts along dimension 0
- output 2: bfloat16 [512, 8192], P('data', 'tp'), parts along dimension 0
There are 2 independent parts. A program takes and returns all parts, laid end to end along the dimension named above; an argument that names none is the same for every part.
All inputs are finite; a program needn't handle non-finite values.
Results may differ from a plain program's by a relative error of at most 0.00645153.
Values are sent between devices in bfloat16 or wider.
A program may use at most 1 GiB of HBM per device.

v0:
```python
import jax
import jax.numpy as jnp
from jax import lax
from jax.sharding import PartitionSpec as P, NamedSharding

EPS = 1e-5


def solution(mesh):
    tp_size = mesh.shape["tp"]

    def local_step(attn_blk, w_blk, resid_blk, gain_blk):
        tok_rows = attn_blk.shape[0]
        d_local = resid_blk.shape[1]
        d_model = d_local * tp_size
        partial = jnp.dot(attn_blk, w_blk, preferred_element_type=jnp.float32).astype(jnp.bfloat16)
        received = lax.all_to_all(partial, "tp", 1, 0, tiled=True)
        projected = jnp.sum(received.reshape(tp_size, tok_rows, d_local), axis=0, dtype=jnp.float32)
        hidden = resid_blk.astype(jnp.float32) + projected
        sq_part = jnp.sum(hidden * hidden, axis=-1, keepdims=True)
        sq_total = lax.psum(sq_part, "tp")
        normed = hidden * lax.rsqrt(sq_total / d_model + EPS) * gain_blk
        return hidden.astype(jnp.bfloat16), normed.astype(jnp.bfloat16)

    return jax.shard_map(
        local_step,
        mesh=mesh,
        in_specs=(P("data", "tp"), P("tp", None), P("data", "tp"), P("tp")),
        out_specs=(P("data", "tp"), P("data", "tp")),
        check_vma=False,
    )
```

profile of v0, /device:TPU:0, one launch (start us, length us, event | category | flops | bytes accessed | tf_op | source)
XLA Modules:
  0.0 80.3 jit_solution(7663970703024951174)
XLA Ops:
  0.6 0.0 copy-start
  0.6 1.2 %copy-done = bf16[256,2048]{1,0:T(8,128)(2,1)S(1)} copy-done((bf16[256,2048]{1,0:T(8,128)(2,1)S(1)}, bf16[256,2048]{1,0:T(8,128)(2,1)}, u32[]{:S(2)}) %copy-start) | copy-done | bytes 1048600
  1.9 15.1 %convolution_convert_fusion = bf16[256,8192]{1,0:T(8,128)(2,1)S(1)} fusion(bf16[256,2048]{1,0:T(8,128)(2,1)S(1)} %copy-done, bf16[2048,8192]{1,0:T(8,128)(2,1)} %param.5), kind=kOutput, calls=%fused_computation | convolution fusion | flops 8592031744 | bytes 38797312 | tf_op jit(solution)/shard_map/dot_general | solution.py:16
  16.9 0.5 copy.9
  17.4 52.5 %all_to_all.13 = bf16[256,4,2048]{2,0,1:T(8,128)(2,1)S(1)} all-to-all(bf16[256,4,2048]{2,0,1:T(8,128)(2,1)S(1)} %bitcast.8), channel_id=1, replica_groups=mesh['data'=2,'tp'=4] {'tp'}, dimensions={1} | all-to-all | bytes 8388608 | tf_op jit(solution)/shard_map/all_to_all | solution.py:17
  70.0 0.0 copy-start.1
  70.0 0.8 convert_reduce_fusion
  70.8 0.4 copy-done.1
  71.2 0.0 copy-start.2
  71.2 0.4 multiply_reduce_fusion
  71.6 5.8 %psum.7 = f32[256,1]{0,1:T(1,128)S(1)} all-reduce(f32[256,1]{0,1:T(1,128)S(1)} %bitcast.10), channel_id=1, replica_groups=mesh['data'=2,'tp'=4] {'tp'}, use_global_device_ids=true, to_apply=%region_2.0 | all-reduce | flops 256 | bytes 2048 | tf_op jit(solution)/shard_map/psum | solution.py:21
  77.4 0.0 copy-done.2
  77.4 2.9 %multiply_convert_fusion = (bf16[256,2048]{1,0:T(8,128)(2,1)}, bf16[256,2048]{1,0:T(8,128)(2,1)}) fusion(f32[2048]{0:T(1024)S(1)} %copy-done.2, f32[256]{0:T(256)S(1)} %bitcast.11, f32[256,2048]{1,0:T(8,128)S(1)} %convert_reduce_fusion, bf16[256,2048]{1,0:T(8,128)(2,1)} %param.6), kind=kLoop, calls=%fused_computation.3 | loop fusion | flops 3145728 | bytes 5252096 | tf_op jit(solution)/shard_map/convert_element_type | solution.py:23
  (1 shorter events, 0.0 us)
Async XLA Ops:
  0.6 1.2 %copy-start = (bf16[256,2048]{1,0:T(8,128)(2,1)S(1)}, bf16[256,2048]{1,0:T(8,128)(2,1)}, u32[]{:S(2)}) copy-start(bf16[256,2048]{1,0:T(8,128)(2,1)} %param.4) | copy-start | bytes 3145732
  70.0 1.2 %copy-start.1 = (bf16[256,2048]{1,0:T(8,128)(2,1)S(1)}, bf16[256,2048]{1,0:T(8,128)(2,1)}, u32[]{:S(2)}) copy-start(bf16[256,2048]{1,0:T(8,128)(2,1)} %param.6) | copy-start | bytes 3145732
  71.2 6.2 %copy-start.2 = (f32[2048]{0:T(1024)S(1)}, f32[2048]{0:T(1024)}, u32[]{:S(2)}) copy-start(f32[2048]{0:T(1024)} %param.7) | copy-start | bytes 24580
where the time goes:
time: 80.6 us; the launch traced here: 80.3 us
  blocking collectives  58.3 us (72%)
  matrix products  15.1 us (19%)
  other arithmetic  4.1 us (5%)
  local copies, waits for them, and re-layouts  2.15 us (3%)
    all_to_all x1, blocking collectives, local_step(): received = lax.all_to_all(partial, 'tp', 1, 0, tiled=True)  52.5 us
    dot_general x1, matrix products, local_step(): jnp.dot(attn_blk, w_blk, preferred_element_type=jnp.float32)  15.1 us
    psum x1, blocking collectives, local_step(): sq_total = lax.psum(sq_part, 'tp')  5.76 us
    convert_element_type x1, other arithmetic, local_step(): return (hidden.astype(jnp.bfloat16), normed.astype(jnp.bfloat16))  2.89 us
    unnamed x6, local copies, waits for them, and re-layouts  1.64 us

commit v1 on v0

v1 whole, which is shorter than its diff:
```python
import functools

import jax
import jax.numpy as jnp
from jax import lax
from jax.experimental import pallas as pl
from jax.experimental.pallas import tpu as pltpu
from jax.sharding import PartitionSpec as P

EPS = 1e-5
MESH = pl.DeviceIdType.MESH
F32, BF16 = jnp.float32, jnp.bfloat16

CW = 256
N_COL = 2
BIG, SMALL = 32, 16


def kernel(d_model, a_hbm, w_hbm, r_hbm, g_hbm, hid_hbm, nrm_hbm,
           a_v, w_v, r_v, g_v, part, recv, own, hid, nrm, st_tx, st_rx,
           a_sem, w_sem, r_sem, g_sem, col_tx, col_rx, row_tx, row_rx, sib_tx, sib_rx, stat_tx, stat_rx, out_sem):
    t = lax.axis_index("tp")
    rows, _ = a_v.shape
    d_loc = own.shape[1]
    per = d_loc // CW
    peers = ((t + 2) % 4, 3 - t, t + 1 - 2 * (t % 2))
    n_big = (rows - 2 * SMALL) // BIG
    blocks = [(n_big * BIG, SMALL), (n_big * BIG + SMALL, SMALL)]
    n_blk = n_big + 2
    c0 = N_COL * CW

    def w_copy(slot, col):
        return pltpu.make_async_copy(w_hbm.at[:, pl.ds(pl.multiple_of(col, CW), CW)], w_v.at[slot], w_sem.at[slot])

    def cross_col(i):
        k = i % 2
        return (peers[0] + (peers[1] - peers[0]) * k) * d_loc + (i // 2) * CW

    def near_col(i):
        return (peers[2] + (t - peers[2]) * (i // per)) * d_loc + (i % per) * CW

    def remote(src, dst, tx, rx, peer):
        return pltpu.make_async_remote_copy(src_ref=src, dst_ref=dst, send_sem=tx, recv_sem=rx,
                                            device_id={"tp": peer}, device_id_type=MESH)

    def col_copy(k, j):
        cols = pl.ds(j * CW, CW)
        return remote(part.at[k, :, cols], recv.at[k, :, cols], col_tx.at[k, j], col_rx.at[k, j], peers[k])

    def row_copy(k, b, row, n):
        sl = (k, pl.ds(row, n), pl.ds(c0, d_loc - c0))
        return remote(part.at[sl], recv.at[sl], row_tx.at[k, b], row_rx.at[k, b], peers[k])

    def sib_copy():
        return remote(part.at[2], recv.at[2], sib_tx, sib_rx, peers[2])

    def stat_copy(k, b):
        return remote(st_tx.at[b], st_rx.at[k, b], stat_tx.at[k, b], stat_rx.at[k, b], peers[k])

    a_copy = pltpu.make_async_copy(a_hbm, a_v, a_sem)
    r_copy = pltpu.make_async_copy(r_hbm, r_v, r_sem)
    g_copy = pltpu.make_async_copy(g_hbm, g_v, g_sem)
    a_copy.start()
    w_copy(0, cross_col(0)).start()
    w_copy(1, cross_col(1)).start()
    barrier = pltpu.get_barrier_semaphore()
    for p in peers:
        pl.semaphore_signal(barrier, inc=1, device_id={"tp": p}, device_id_type=MESH)
    for i in range(2, 2 * per):
        w_copy(i, cross_col(i)).start()
    pl.semaphore_wait(barrier, 3)
    a_copy.wait()

    def chunk(slot, col):
        w_copy(slot, col).wait()
        return jnp.dot(a_v[...], w_v[slot], preferred_element_type=F32)

    def cross(i, by_col):
        k, j = i % 2, i // 2
        part[k, :, pl.ds(pl.multiple_of(j * CW, CW), CW)] = chunk(i, cross_col(i)).astype(BF16)
        w_copy(2 * per + i, near_col(i)).start()

    for i in range(2 * N_COL):
        cross(i, True)
        col_copy(i % 2, i // 2).start()

    @pl.loop(2 * N_COL, 2 * per)
    def _(i):
        cross(i, False)

    @pl.loop(0, n_big)
    def _(b):
        row = pl.multiple_of(b * BIG, BIG)
        row_copy(0, b, row, BIG).start()
        row_copy(1, b, row, BIG).start()

    for q, (row, n) in enumerate(blocks):
        row_copy(0, n_big + q, row, n).start()
        row_copy(1, n_big + q, row, n).start()
    r_copy.start()
    g_copy.start()

    @pl.loop(0, per)
    def _(j):
        part[2, :, pl.ds(pl.multiple_of(j * CW, CW), CW)] = chunk(2 * per + j, near_col(j)).astype(BF16)

    sib_copy().start()

    @pl.loop(0, per)
    def _(j):
        own[:, pl.ds(pl.multiple_of(j * CW, CW), CW)] = chunk(3 * per + j, near_col(per + j))

    r_copy.wait()
    g_copy.wait()
    sib_copy().wait_recv()
    for j in range(N_COL):
        for k in range(2):
            col_copy(k, j).wait_recv()

    lane = lax.broadcasted_iota(jnp.int32, (8, 128), 1)
    sub = lax.broadcasted_iota(jnp.int32, (8, 128), 0)

    def reduce_block(b, row, n):
        row_copy(0, b, row, n).wait_recv()
        row_copy(1, b, row, n).wait_recv()
        sl = pl.ds(row, n)
        h = own[sl, :] + recv[0, sl, :].astype(F32) + recv[1, sl, :].astype(F32) + recv[2, sl, :].astype(F32)
        h = r_v[sl, :].astype(F32) + h
        own[sl, :] = h
        hid[sl, :] = h.astype(BF16)
        s = jnp.sum(h * h, axis=1, keepdims=True)
        line = jnp.zeros((8, 128), F32)
        for q in range(n // 8):
            line = line + jnp.where(lane == sub + 8 * q, s[8 * q:8 * q + 8, :], 0.0)
        st_tx[b] = jnp.sum(line, axis=0, keepdims=True)
        for k in range(3):
            stat_copy(k, b).start()
        pltpu.make_async_copy(hid.at[sl, :], hid_hbm.at[sl, :], out_sem.at[0, b]).start()

    def norm_block(b, row, n):
        for k in range(3):
            stat_copy(k, b).wait_recv()
        tot = (st_tx[b] + st_rx[2, b]) + (st_rx[0, b] + st_rx[1, b])
        scale = lax.rsqrt(tot / d_model + EPS)
        scale = jnp.broadcast_to(scale, (8, 128))
        for q in range(n // 8):
            sl = pl.ds(row + 8 * q, 8)
            col = jnp.sum(jnp.where(lane == sub + 8 * q, scale, 0.0), axis=1, keepdims=True)
            own[sl, :] = own[sl, :] * col * g_v[...]
        sl = pl.ds(row, n)
        nrm[sl, :] = own[sl, :].astype(BF16)
        pltpu.make_async_copy(nrm.at[sl, :], nrm_hbm.at[sl, :], out_sem.at[1, b]).start()

    reduce_block(0, 0, BIG)

    @pl.loop(1, n_big)
    def _(b):
        row = pl.multiple_of(b * BIG, BIG)
        reduce_block(b, row, BIG)
        norm_block(b - 1, pl.multiple_of(row - BIG, BIG), BIG)

    (row_s, n_s), (row_l, n_l) = blocks
    reduce_block(n_big, row_s, n_s)
    norm_block(n_big - 1, row_s - BIG, BIG)
    reduce_block(n_big + 1, row_l, n_l)
    norm_block(n_big, row_s, n_s)
    norm_block(n_big + 1, row_l, n_l)

    for j in range(N_COL):
        for k in range(2):
            col_copy(k, j).wait_send()
    sib_copy().wait_send()

    def drain(b, row, n):
        sl = pl.ds(row, n)
        row_copy(0, b, row, n).wait_send()
        row_copy(1, b, row, n).wait_send()
        for k in range(3):
            stat_copy(k, b).wait_send()
        pltpu.make_async_copy(hid.at[sl, :], hid_hbm.at[sl, :], out_sem.at[0, b]).wait()
        pltpu.make_async_copy(nrm.at[sl, :], nrm_hbm.at[sl, :], out_sem.at[1, b]).wait()

    @pl.loop(0, n_big)
    def _(b):
        drain(b, pl.multiple_of(b * BIG, BIG), BIG)

    drain(n_big, row_s, n_s)
    drain(n_big + 1, row_l, n_l)


def solution(mesh):
    tp = mesh.shape["tp"]

    def local_step(a, w, r, g):
        rows, depth = a.shape
        d_loc = r.shape[1]
        per = d_loc // CW
        n_blk = (rows - 2 * SMALL) // BIG + 2
        any_spec = pl.BlockSpec(memory_space=pl.ANY)
        dma = pltpu.SemaphoreType.DMA
        return pl.pallas_call(
            functools.partial(kernel, d_loc * tp),
            out_shape=(jax.ShapeDtypeStruct((rows, d_loc), BF16),) * 2,
            in_specs=[any_spec] * 4,
            out_specs=(any_spec,) * 2,
            scratch_shapes=[
                pltpu.VMEM((rows, depth), BF16),
                pltpu.VMEM((4 * per, depth, CW), BF16),
                pltpu.VMEM((rows, d_loc), BF16),
                pltpu.VMEM((1, d_loc), F32),
                pltpu.VMEM((3, rows, d_loc), BF16),
                pltpu.VMEM((3, rows, d_loc), BF16),
                pltpu.VMEM((rows, d_loc), F32),
                pltpu.VMEM((rows, d_loc), BF16),
                pltpu.VMEM((rows, d_loc), BF16),
                pltpu.VMEM((n_blk, 1, 128), F32),
                pltpu.VMEM((3, n_blk, 1, 128), F32),
                dma, dma((4 * per,)), dma, dma,
                dma((2, N_COL)), dma((2, N_COL)), dma((2, n_blk)), dma((2, n_blk)), dma, dma,
                dma((3, n_blk)), dma((3, n_blk)), dma((2, n_blk)),
            ],
            compiler_params=pltpu.CompilerParams(
                collective_id=0, has_side_effects=True, vmem_limit_bytes=56 * 1024 * 1024),
            cost_estimate=pl.CostEstimate(flops=2 * rows * depth * d_loc * tp, transcendentals=0,
                                          bytes_accessed=2 * depth * d_loc * tp),
        )(a, w, r, g.reshape(1, d_loc))

    return jax.shard_map(
        local_step,
        mesh=mesh,
        in_specs=(P("data", "tp"), P("tp", None), P("data", "tp"), P("tp")),
        out_specs=(P("data", "tp"), P("data", "tp")),
        check_vma=False,
    )
```

time: 80.6 us -> 70.3 us (0.87)
  Pallas kernels: 0 us -> 64.8 us
  blocking collectives: 58.3 us -> 0 us
  matrix products: 15.1 us -> 0 us
  other arithmetic: 4.1 us -> 0 us
  local copies, waits for them, and re-layouts: 2.15 us -> 4.61 us
    pallas_call x0 -> x1, Pallas kernels: none -> 64.8 us  [local_step(): pl.pallas_call(functools.partial(kernel, d_loc * tp), out_shape=(jax.Shap...]
    all_to_all x1 -> x0, blocking collectives: 52.5 us -> none  [local_step(): received = lax.all_to_all(partial, 'tp', 1, 0, tiled=True)]
    dot_general x1 -> x0, matrix products: 15.1 us -> none  [local_step(): jnp.dot(attn_blk, w_blk, preferred_element_type=jnp.float32)]
    psum x1 -> x0, blocking collectives: 5.76 us -> none  [local_step(): sq_total = lax.psum(sq_part, 'tp')]
    unnamed x6 -> x2, local copies, waits for them, and re-layouts: 1.64 us -> 4.61 us
    convert_element_type x1 -> x0, other arithmetic: 2.89 us -> none  [local_step(): return (hidden.astype(jnp.bfloat16), normed.astype(jnp.bfloat16))]
    reduce_sum x2 -> x0, other arithmetic: 1.2 us -> none  [the longest x1 0.8 us: local_step(): jnp.sum(received.reshape(tp_size, tok_rows, d_local), axis=0, dtype=jnp.f...]
where the time goes in v1:
time: 70.3 us; the launch traced here: 70.1 us
  Pallas kernels  64.8 us (92%)
  local copies, waits for them, and re-layouts  4.61 us (7%)
    pallas_call x1, Pallas kernels, local_step(): pl.pallas_call(functools.partial(kernel, d_loc * tp), out_shape=(jax.Shap...  64.8 us
    unnamed x2, local copies, waits for them, and re-layouts  4.61 us

profile of v1, /device:TPU:0, one launch (start us, length us, event | category | flops | bytes accessed | tf_op | source)
XLA Modules:
  0.0 70.1 jit_solution(14842683902266604918)
XLA Ops:
  0.6 64.8 %shard_map.59 = (bf16[256,2048]{1,0:T(8,128)(2,1)}, bf16[256,2048]{1,0:T(8,128)(2,1)}) custom-call(bf16[256,2048]{1,0:T(8,128)(2,1)} %a_hbm.1, bf16[2048,8192]{1,0:T(8,128)(2,1)} %w_hbm.1, bf16[256,2048]{1,0:T(8,128)(2,1)} %r_hbm.1, f32[1,2048]{1,0:T(1,128)} %bitcast.1), custom_call_target="tpu_custom_call" | custom-call | flops 8589934592 | bytes 33554432 | tf_op jit(solution)/shard_map/pallas_call | solution.py:201
  65.5 2.3 %copy.8 = bf16[256,2048]{1,0:T(8,128)(2,1)} copy(bf16[256,2048]{1,0:T(8,128)(2,1)} %get-tuple-element.4) | data formatting | bytes 2097152
  67.8 2.3 %copy.9 = bf16[256,2048]{1,0:T(8,128)(2,1)} copy(bf16[256,2048]{1,0:T(8,128)(2,1)} %get-tuple-element.5) | data formatting | bytes 2097152

commit v2 on v1

--- a/solution.py
+++ b/solution.py
@@ -14,6 +14,7 @@
 CW = 256
 N_COL = 2
 BIG, SMALL = 32, 16
+AHEAD = 2
 
 
 def kernel(d_model, a_hbm, w_hbm, r_hbm, g_hbm, hid_hbm, nrm_hbm,
@@ -88,15 +89,16 @@
     def _(i):
         cross(i, False)
 
-    @pl.loop(0, n_big)
-    def _(b):
-        row = pl.multiple_of(b * BIG, BIG)
-        row_copy(0, b, row, BIG).start()
-        row_copy(1, b, row, BIG).start()
-
-    for q, (row, n) in enumerate(blocks):
-        row_copy(0, n_big + q, row, n).start()
-        row_copy(1, n_big + q, row, n).start()
+    def send_block(b, row, n):
+        row_copy(0, b, row, n).start()
+        row_copy(1, b, row, n).start()
+
+    def sent_block(b, row, n):
+        row_copy(0, b, row, n).wait_send()
+        row_copy(1, b, row, n).wait_send()
+
+    for b in range(AHEAD):
+        send_block(b, b * BIG, BIG)
     r_copy.start()
     g_copy.start()
 
@@ -151,20 +153,34 @@
         nrm[sl, :] = own[sl, :].astype(BF16)
         pltpu.make_async_copy(nrm.at[sl, :], nrm_hbm.at[sl, :], out_sem.at[1, b]).start()
 
+    (row_s, n_s), (row_l, n_l) = blocks
+
+    sent_block(0, 0, BIG)
+    send_block(AHEAD, AHEAD * BIG, BIG)
     reduce_block(0, 0, BIG)
 
-    @pl.loop(1, n_big)
+    @pl.loop(1, n_big - AHEAD)
     def _(b):
         row = pl.multiple_of(b * BIG, BIG)
+        sent_block(b, row, BIG)
+        send_block(b + AHEAD, pl.multiple_of(row + AHEAD * BIG, BIG), BIG)
         reduce_block(b, row, BIG)
         norm_block(b - 1, pl.multiple_of(row - BIG, BIG), BIG)
 
-    (row_s, n_s), (row_l, n_l) = blocks
+    for q in range(2):
+        b = n_big - 2 + q
+        sent_block(b, b * BIG, BIG)
+        send_block(n_big + q, *blocks[q])
+        reduce_block(b, b * BIG, BIG)
+        norm_block(b - 1, b * BIG - BIG, BIG)
+
     reduce_block(n_big, row_s, n_s)
     norm_block(n_big - 1, row_s - BIG, BIG)
     reduce_block(n_big + 1, row_l, n_l)
     norm_block(n_big, row_s, n_s)
     norm_block(n_big + 1, row_l, n_l)
+    sent_block(n_big, row_s, n_s)
+    sent_block(n_big + 1, row_l, n_l)
 
     for j in range(N_COL):
         for k in range(2):
@@ -173,8 +189,6 @@
 
     def drain(b, row, n):
         sl = pl.ds(row, n)
-        row_copy(0, b, row, n).wait_send()
-        row_copy(1, b, row, n).wait_send()
         for k in range(3):
             stat_copy(k, b).wait_send()
         pltpu.make_async_copy(hid.at[sl, :], hid_hbm.at[sl, :], out_sem.at[0, b]).wait()

time: 70.3 us -> 62.7 us (0.89)
  Pallas kernels: 64.8 us -> 57.3 us
    pallas_call x1, Pallas kernels: 64.8 us -> 57.3 us  [local_step(): pl.pallas_call(functools.partial(kernel, d_loc * tp), out_shape=(jax.Shap...]
where the time goes in v2:
time: 62.7 us; the launch traced here: 62.6 us
  Pallas kernels  57.3 us (91%)
  local copies, waits for them, and re-layouts  4.61 us (7%)
  between operations  0.64 us (1%)
    pallas_call x1, Pallas kernels, local_step(): pl.pallas_call(functools.partial(kernel, d_loc * tp), out_shape=(jax.Shap...  57.3 us
    unnamed x2, local copies, waits for them, and re-layouts  4.61 us

profile of v2, /device:TPU:0, one launch (start us, length us, event | category | flops | bytes accessed | tf_op | source)
XLA Modules:
  0.0 62.6 jit_solution(17867482175850289159)
XLA Ops:
  0.6 57.3 %shard_map.59 = (bf16[256,2048]{1,0:T(8,128)(2,1)}, bf16[256,2048]{1,0:T(8,128)(2,1)}) custom-call(bf16[256,2048]{1,0:T(8,128)(2,1)} %a_hbm.1, bf16[2048,8192]{1,0:T(8,128)(2,1)} %w_hbm.1, bf16[256,2048]{1,0:T(8,128)(2,1)} %r_hbm.1, f32[1,2048]{1,0:T(1,128)} %bitcast.1), custom_call_target="tpu_custom_call" | custom-call | flops 8589934592 | bytes 33554432 | tf_op jit(solution)/shard_map/pallas_call | solution.py:215
  58.0 2.3 %copy.8 = bf16[256,2048]{1,0:T(8,128)(2,1)} copy(bf16[256,2048]{1,0:T(8,128)(2,1)} %get-tuple-element.4) | data formatting | bytes 2097152
  60.3 2.3 %copy.9 = bf16[256,2048]{1,0:T(8,128)(2,1)} copy(bf16[256,2048]{1,0:T(8,128)(2,1)} %get-tuple-element.5) | data formatting | bytes 2097152

commit v3 on v2

--- a/solution.py
+++ b/solution.py
@@ -17,9 +17,9 @@
 AHEAD = 2
 
 
-def kernel(d_model, a_hbm, w_hbm, r_hbm, g_hbm, hid_hbm, nrm_hbm,
-           a_v, w_v, r_v, g_v, part, recv, own, hid, nrm, st_tx, st_rx,
-           a_sem, w_sem, r_sem, g_sem, col_tx, col_rx, row_tx, row_rx, sib_tx, sib_rx, stat_tx, stat_rx, out_sem):
+def kernel(d_model, a_hbm, w_hbm, r_hbm, g_hbm, hid, nrm,
+           a_v, w_v, r_v, g_v, part, recv, own, st_tx, st_rx,
+           a_sem, w_sem, r_sem, g_sem, col_tx, col_rx, row_tx, row_rx, sib_tx, sib_rx, stat_tx, stat_rx):
     t = lax.axis_index("tp")
     rows, _ = a_v.shape
     d_loc = own.shape[1]
@@ -137,7 +137,6 @@
         st_tx[b] = jnp.sum(line, axis=0, keepdims=True)
         for k in range(3):
             stat_copy(k, b).start()
-        pltpu.make_async_copy(hid.at[sl, :], hid_hbm.at[sl, :], out_sem.at[0, b]).start()
 
     def norm_block(b, row, n):
         for k in range(3):
@@ -151,7 +150,6 @@
             own[sl, :] = own[sl, :] * col * g_v[...]
         sl = pl.ds(row, n)
         nrm[sl, :] = own[sl, :].astype(BF16)
-        pltpu.make_async_copy(nrm.at[sl, :], nrm_hbm.at[sl, :], out_sem.at[1, b]).start()
 
     (row_s, n_s), (row_l, n_l) = blocks
 
@@ -187,19 +185,18 @@
             col_copy(k, j).wait_send()
     sib_copy().wait_send()
 
-    def drain(b, row, n):
-        sl = pl.ds(row, n)
+    @pl.loop(0, n_big + 2)
+    def _(b):
         for k in range(3):
             stat_copy(k, b).wait_send()
-        pltpu.make_async_copy(hid.at[sl, :], hid_hbm.at[sl, :], out_sem.at[0, b]).wait()
-        pltpu.make_async_copy(nrm.at[sl, :], nrm_hbm.at[sl, :], out_sem.at[1, b]).wait()
-
-    @pl.loop(0, n_big)
-    def _(b):
-        drain(b, pl.multiple_of(b * BIG, BIG), BIG)
-
-    drain(n_big, row_s, n_s)
-    drain(n_big + 1, row_l, n_l)
+
+
+def put(hid, nrm, hid_hbm, nrm_hbm, sem):
+    copies = (pltpu.make_async_copy(hid, hid_hbm, sem.at[0]), pltpu.make_async_copy(nrm, nrm_hbm, sem.at[1]))
+    for c in copies:
+        c.start()
+    for c in copies:
+        c.wait()
 
 
 def solution(mesh):
@@ -210,13 +207,14 @@
         d_loc = r.shape[1]
         per = d_loc // CW
         n_blk = (rows - 2 * SMALL) // BIG + 2
-        any_spec = pl.BlockSpec(memory_space=pl.ANY)
+        hbm = pl.BlockSpec(memory_space=pltpu.HBM)
+        vmem = pl.BlockSpec(memory_space=pltpu.VMEM)
         dma = pltpu.SemaphoreType.DMA
-        return pl.pallas_call(
+        hid, nrm = pl.pallas_call(
             functools.partial(kernel, d_loc * tp),
-            out_shape=(jax.ShapeDtypeStruct((rows, d_loc), BF16),) * 2,
-            in_specs=[any_spec] * 4,
-            out_specs=(any_spec,) * 2,
+            out_shape=(pltpu.VMEM((rows, d_loc), BF16),) * 2,
+            in_specs=[hbm] * 4,
+            out_specs=(vmem,) * 2,
             scratch_shapes=[
                 pltpu.VMEM((rows, depth), BF16),
                 pltpu.VMEM((4 * per, depth, CW), BF16),
@@ -225,19 +223,25 @@
                 pltpu.VMEM((3, rows, d_loc), BF16),
                 pltpu.VMEM((3, rows, d_loc), BF16),
                 pltpu.VMEM((rows, d_loc), F32),
-                pltpu.VMEM((rows, d_loc), BF16),
-                pltpu.VMEM((rows, d_loc), BF16),
                 pltpu.VMEM((n_blk, 1, 128), F32),
                 pltpu.VMEM((3, n_blk, 1, 128), F32),
                 dma, dma((4 * per,)), dma, dma,
                 dma((2, N_COL)), dma((2, N_COL)), dma((2, n_blk)), dma((2, n_blk)), dma, dma,
-                dma((3, n_blk)), dma((3, n_blk)), dma((2, n_blk)),
+                dma((3, n_blk)), dma((3, n_blk)),
             ],
             compiler_params=pltpu.CompilerParams(
-                collective_id=0, has_side_effects=True, vmem_limit_bytes=56 * 1024 * 1024),
+                collective_id=0, has_side_effects=True, vmem_limit_bytes=64946176),
             cost_estimate=pl.CostEstimate(flops=2 * rows * depth * d_loc * tp, transcendentals=0,
                                           bytes_accessed=2 * depth * d_loc * tp),
         )(a, w, r, g.reshape(1, d_loc))
+        return pl.pallas_call(
+            put,
+            out_shape=(jax.ShapeDtypeStruct((rows, d_loc), BF16),) * 2,
+            in_specs=[vmem] * 2,
+            out_specs=(hbm,) * 2,
+            scratch_shapes=[dma((2,))],
+            compiler_params=pltpu.CompilerParams(vmem_limit_bytes=1024 * 1024),
+        )(hid, nrm)
 
     return jax.shard_map(
         local_step,

time: 62.7 us -> 58.7 us (0.936)
  local copies, waits for them, and re-layouts: 4.61 us -> 0 us
    unnamed x2 -> x0, local copies, waits for them, and re-layouts: 4.61 us -> none
    pallas_call x1 -> x2, Pallas kernels: 57.3 us -> 57.9 us  [the longest x1 56.6 us: local_step(): pl.pallas_call(functools.partial(kernel, d_loc * tp), out_shape=(pltpu.VM...]
where the time goes in v3:
time: 58.7 us; the launch traced here: 58.6 us
  Pallas kernels  57.9 us (99%)
  between operations  0.64 us (1%)
    pallas_call x1, Pallas kernels, local_step(): pl.pallas_call(functools.partial(kernel, d_loc * tp), out_shape=(pltpu.VM...  56.6 us
    pallas_call x1, Pallas kernels, local_step(): pl.pallas_call(put, out_shape=(jax.ShapeDtypeStruct((rows, d_loc), BF16),...  1.33 us

profile of v3, /device:TPU:0, one launch (start us, length us, event | category | flops | bytes accessed | tf_op | source)
XLA Modules:
  0.0 58.6 jit_solution(10404240290381977609)
XLA Ops:
  0.6 56.6 %shard_map.59 = (bf16[256,2048]{1,0:T(8,128)(2,1)S(1)}, bf16[256,2048]{1,0:T(8,128)(2,1)S(1)}) custom-call(bf16[256,2048]{1,0:T(8,128)(2,1)} %a_hbm.1, bf16[2048,8192]{1,0:T(8,128)(2,1)} %w_hbm.1, bf16[256,2048]{1,0:T(8,128)(2,1)} %r_hbm.1, f32[1,2048]{1,0:T(1,128)} %bitcast.1), custom_call_target="tpu_custom_call" | custom-call | flops 8589934592 | bytes 33554432 | tf_op jit(solution)/shard_map/pallas_call | solution.py:213
  57.3 1.3 %shard_map.60 = (bf16[256,2048]{1,0:T(8,128)(2,1)}, bf16[256,2048]{1,0:T(8,128)(2,1)}) custom-call(bf16[256,2048]{1,0:T(8,128)(2,1)S(1)} %get-tuple-element.4.hid, bf16[256,2048]{1,0:T(8,128)(2,1)S(1)} %get-tuple-element.5.nrm), custom_call_target="tpu_custom_call" | custom-call | tf_op jit(solution)/shard_map/pallas_call | solution.py:237

commit v4 on v3

--- a/solution.py
+++ b/solution.py
@@ -14,12 +14,14 @@
 CW = 256
 N_COL = 2
 BIG, SMALL = 32, 16
+DEPTH = 4
+PUT = 4
 AHEAD = 2
 
 
 def kernel(d_model, a_hbm, w_hbm, r_hbm, g_hbm, hid, nrm,
            a_v, w_v, r_v, g_v, part, recv, own, st_tx, st_rx,
-           a_sem, w_sem, r_sem, g_sem, col_tx, col_rx, row_tx, row_rx, sib_tx, sib_rx, stat_tx, stat_rx):
+           a_sem, w0_sem, w_sem, r_sem, g_sem, first_tx, first_rx, col_tx, col_rx, row_tx, row_rx, sib_tx, sib_rx, stat_tx, stat_rx):
     t = lax.axis_index("tp")
     rows, _ = a_v.shape
     d_loc = own.shape[1]
@@ -58,36 +60,80 @@
     def stat_copy(k, b):
         return remote(st_tx.at[b], st_rx.at[k, b], stat_tx.at[k, b], stat_rx.at[k, b], peers[k])
 
-    a_copy = pltpu.make_async_copy(a_hbm, a_v, a_sem)
+    half, lanes = rows // 2, 128
+
+    def a_copy(q):
+        sl = pl.ds(q * half, half)
+        return pltpu.make_async_copy(a_hbm.at[sl, :], a_v.at[sl, :], a_sem.at[q])
+
+    def w0_copy(q, first, n):
+        src = w_hbm.at[:, pl.ds(pl.multiple_of(cross_col(0) + first, lanes), n)]
+        return pltpu.make_async_copy(src, w_v.at[0, :, pl.ds(first, n)], w0_sem.at[q])
+
+    def w_start(i):
+        if isinstance(i, int):
+            w_copy(i, cross_col(i) if i < 2 * per else near_col(i - 2 * per)).start()
+            return
+
+        @pl.when(i < 2 * per)
+        def _():
+            w_copy(i, cross_col(i)).start()
+
+        @pl.when((i >= 2 * per) & (i < 4 * per))
+        def _():
+            w_copy(i, near_col(i - 2 * per)).start()
+
     r_copy = pltpu.make_async_copy(r_hbm, r_v, r_sem)
     g_copy = pltpu.make_async_copy(g_hbm, g_v, g_sem)
-    a_copy.start()
-    w_copy(0, cross_col(0)).start()
-    w_copy(1, cross_col(1)).start()
+    a_copy(0).start()
+    w0_copy(0, 0, lanes).start()
+    a_copy(1).start()
+    w0_copy(1, lanes, CW - lanes).start()
     barrier = pltpu.get_barrier_semaphore()
     for p in peers:
         pl.semaphore_signal(barrier, inc=1, device_id={"tp": p}, device_id_type=MESH)
-    for i in range(2, 2 * per):
-        w_copy(i, cross_col(i)).start()
-    pl.semaphore_wait(barrier, 3)
-    a_copy.wait()
-
-    def chunk(slot, col):
-        w_copy(slot, col).wait()
-        return jnp.dot(a_v[...], w_v[slot], preferred_element_type=F32)
-
-    def cross(i, by_col):
-        k, j = i % 2, i // 2
-        part[k, :, pl.ds(pl.multiple_of(j * CW, CW), CW)] = chunk(i, cross_col(i)).astype(BF16)
-        w_copy(2 * per + i, near_col(i)).start()
-
-    for i in range(2 * N_COL):
-        cross(i, True)
+
+    def dot(lhs, rhs):
+        return jnp.dot(lhs, rhs, preferred_element_type=F32)
+
+    pieces = ((pl.ds(0, half), pl.ds(0, lanes)), (pl.ds(half, half), pl.ds(0, lanes)),
+              (pl.ds(0, rows), pl.ds(lanes, CW - lanes)))
+
+    def piece_copy(q):
+        sl = (0, *pieces[q])
+        return remote(part.at[sl], recv.at[sl], first_tx.at[q], first_rx.at[q], peers[0])
+
+    for q, (r_sl, c_sl) in enumerate(pieces):
+        if q == 0:
+            a_copy(0).wait()
+            w0_copy(0, 0, lanes).wait()
+            for i in range(1, DEPTH):
+                w_start(i)
+        elif q == 1:
+            a_copy(1).wait()
+        else:
+            w0_copy(1, lanes, CW - lanes).wait()
+            w_start(DEPTH)
+        part[0, r_sl, c_sl] = dot(a_v[r_sl, :], w_v[0, :, c_sl]).astype(BF16)
+        if q == 0:
+            pl.semaphore_wait(barrier, 3)
+        piece_copy(q).start()
+
+    def chunk(i, col):
+        w_copy(i, col).wait()
+        w_start(i + DEPTH)
+        return dot(a_v[...], w_v[i])
+
+    def cross(i):
+        part[i % 2, :, pl.ds(pl.multiple_of((i // 2) * CW, CW), CW)] = chunk(i, cross_col(i)).astype(BF16)
+
+    for i in range(1, 2 * N_COL):
+        cross(i)
         col_copy(i % 2, i // 2).start()
 
     @pl.loop(2 * N_COL, 2 * per)
     def _(i):
-        cross(i, False)
+        cross(i)
 
     def send_block(b, row, n):
         row_copy(0, b, row, n).start()
@@ -115,9 +161,10 @@
     r_copy.wait()
     g_copy.wait()
     sib_copy().wait_recv()
-    for j in range(N_COL):
-        for k in range(2):
-            col_copy(k, j).wait_recv()
+    for q in range(len(pieces)):
+        piece_copy(q).wait_recv()
+    for i in range(1, 2 * N_COL):
+        col_copy(i % 2, i // 2).wait_recv()
 
     lane = lax.broadcasted_iota(jnp.int32, (8, 128), 1)
     sub = lax.broadcasted_iota(jnp.int32, (8, 128), 0)
@@ -180,9 +227,10 @@
     sent_block(n_big, row_s, n_s)
     sent_block(n_big + 1, row_l, n_l)
 
-    for j in range(N_COL):
-        for k in range(2):
-            col_copy(k, j).wait_send()
+    for q in range(len(pieces)):
+        piece_copy(q).wait_send()
+    for i in range(1, 2 * N_COL):
+        col_copy(i % 2, i // 2).wait_send()
     sib_copy().wait_send()
 
     @pl.loop(0, n_big + 2)
@@ -192,7 +240,12 @@
 
 
 def put(hid, nrm, hid_hbm, nrm_hbm, sem):
-    copies = (pltpu.make_async_copy(hid, hid_hbm, sem.at[0]), pltpu.make_async_copy(nrm, nrm_hbm, sem.at[1]))
+    n = hid.shape[0] // PUT
+    copies = []
+    for q in range(PUT):
+        sl = pl.ds(q * n, n)
+        copies.append(pltpu.make_async_copy(hid.at[sl, :], hid_hbm.at[sl, :], sem.at[0, q]))
+        copies.append(pltpu.make_async_copy(nrm.at[sl, :], nrm_hbm.at[sl, :], sem.at[1, q]))
     for c in copies:
         c.start()
     for c in copies:
@@ -225,7 +278,7 @@
                 pltpu.VMEM((rows, d_loc), F32),
                 pltpu.VMEM((n_blk, 1, 128), F32),
                 pltpu.VMEM((3, n_blk, 1, 128), F32),
-                dma, dma((4 * per,)), dma, dma,
+                dma((2,)), dma((2,)), dma((4 * per,)), dma, dma, dma((3,)), dma((3,)),
                 dma((2, N_COL)), dma((2, N_COL)), dma((2, n_blk)), dma((2, n_blk)), dma, dma,
                 dma((3, n_blk)), dma((3, n_blk)),
             ],
@@ -239,7 +292,7 @@
             out_shape=(jax.ShapeDtypeStruct((rows, d_loc), BF16),) * 2,
             in_specs=[vmem] * 2,
             out_specs=(hbm,) * 2,
-            scratch_shapes=[dma((2,))],
+            scratch_shapes=[dma((2, PUT))],
             compiler_params=pltpu.CompilerParams(vmem_limit_bytes=1024 * 1024),
         )(hid, nrm)
 

time: 58.7 us -> 58.1 us (0.990)
    pallas_call x1, Pallas kernels: 56.6 us -> 56 us  [local_step(): pl.pallas_call(functools.partial(kernel, d_loc * tp), out_shape=(pltpu.VM...]
where the time goes in v4:
time: 58.1 us; the launch traced here: 58 us
  Pallas kernels  57.4 us (99%)
  between operations  0.64 us (1%)
    pallas_call x1, Pallas kernels, local_step(): pl.pallas_call(functools.partial(kernel, d_loc * tp), out_shape=(pltpu.VM...  56 us
    pallas_call x1, Pallas kernels, local_step(): pl.pallas_call(put, out_shape=(jax.ShapeDtypeStruct((rows, d_loc), BF16),...  1.38 us

profile of v4, /device:TPU:0, one launch (start us, length us, event | category | flops | bytes accessed | tf_op | source)
XLA Modules:
  0.0 58.0 jit_solution(5061170839526395897)
XLA Ops:
  0.6 56.0 %shard_map.59 = (bf16[256,2048]{1,0:T(8,128)(2,1)S(1)}, bf16[256,2048]{1,0:T(8,128)(2,1)S(1)}) custom-call(bf16[256,2048]{1,0:T(8,128)(2,1)} %a_hbm.1, bf16[2048,8192]{1,0:T(8,128)(2,1)} %w_hbm.1, bf16[256,2048]{1,0:T(8,128)(2,1)} %r_hbm.1, f32[1,2048]{1,0:T(1,128)} %bitcast.1), custom_call_target="tpu_custom_call" | custom-call | flops 8589934592 | bytes 33554432 | tf_op jit(solution)/shard_map/pallas_call | solution.py:266
  56.6 1.4 %shard_map.60 = (bf16[256,2048]{1,0:T(8,128)(2,1)}, bf16[256,2048]{1,0:T(8,128)(2,1)}) custom-call(bf16[256,2048]{1,0:T(8,128)(2,1)S(1)} %get-tuple-element.4.hid, bf16[256,2048]{1,0:T(8,128)(2,1)S(1)} %get-tuple-element.5.nrm), custom_call_target="tpu_custom_call" | custom-call | tf_op jit(solution)/shard_map/pallas_call | solution.py:290

commit v5 on v4

--- a/solution.py
+++ b/solution.py
@@ -15,7 +15,7 @@
 N_COL = 2
 BIG, SMALL = 32, 16
 DEPTH = 4
-PUT = 4
+PUT = 1
 AHEAD = 2
 
 
@@ -220,8 +220,8 @@
         norm_block(b - 1, b * BIG - BIG, BIG)
 
     reduce_block(n_big, row_s, n_s)
+    reduce_block(n_big + 1, row_l, n_l)
     norm_block(n_big - 1, row_s - BIG, BIG)
-    reduce_block(n_big + 1, row_l, n_l)
     norm_block(n_big, row_s, n_s)
     norm_block(n_big + 1, row_l, n_l)
     sent_block(n_big, row_s, n_s)

time: 58.1 us -> 57.4 us (0.988)
  Pallas kernels: 57.4 us -> 56.6 us
    pallas_call x1, Pallas kernels: 56 us -> 55.3 us  [local_step(): pl.pallas_call(functools.partial(kernel, d_loc * tp), out_shape=(pltpu.VM...]
where the time goes in v5:
time: 57.4 us; the launch traced here: 57.3 us
  Pallas kernels  56.6 us (99%)
  between operations  0.64 us (1%)
    pallas_call x1, Pallas kernels, local_step(): pl.pallas_call(functools.partial(kernel, d_loc * tp), out_shape=(pltpu.VM...  55.3 us
    pallas_call x1, Pallas kernels, local_step(): pl.pallas_call(put, out_shape=(jax.ShapeDtypeStruct((rows, d_loc), BF16),...  1.33 us

profile of v5, /device:TPU:0, one launch (start us, length us, event | category | flops | bytes accessed | tf_op | source)
XLA Modules:
  0.0 57.3 jit_solution(1379205549086036357)
XLA Ops:
  0.6 55.3 %shard_map.59 = (bf16[256,2048]{1,0:T(8,128)(2,1)S(1)}, bf16[256,2048]{1,0:T(8,128)(2,1)S(1)}) custom-call(bf16[256,2048]{1,0:T(8,128)(2,1)} %a_hbm.1, bf16[2048,8192]{1,0:T(8,128)(2,1)} %w_hbm.1, bf16[256,2048]{1,0:T(8,128)(2,1)} %r_hbm.1, f32[1,2048]{1,0:T(1,128)} %bitcast.1), custom_call_target="tpu_custom_call" | custom-call | flops 8589934592 | bytes 33554432 | tf_op jit(solution)/shard_map/pallas_call | solution.py:266
  55.9 1.3 %shard_map.60 = (bf16[256,2048]{1,0:T(8,128)(2,1)}, bf16[256,2048]{1,0:T(8,128)(2,1)}) custom-call(bf16[256,2048]{1,0:T(8,128)(2,1)S(1)} %get-tuple-element.4.hid, bf16[256,2048]{1,0:T(8,128)(2,1)S(1)} %get-tuple-element.5.nrm), custom_call_target="tpu_custom_call" | custom-call | tf_op jit(solution)/shard_map/pallas_call | solution.py:290

commit v6 on v5

--- a/solution.py
+++ b/solution.py
@@ -13,7 +13,8 @@
 
 CW = 256
 N_COL = 2
-BIG, SMALL = 32, 16
+BLOCKS = (64, 64, 64, 32, 16, 16)
+SUB = 16
 DEPTH = 4
 PUT = 1
 AHEAD = 2
@@ -27,9 +28,8 @@
     d_loc = own.shape[1]
     per = d_loc // CW
     peers = ((t + 2) % 4, 3 - t, t + 1 - 2 * (t % 2))
-    n_big = (rows - 2 * SMALL) // BIG
-    blocks = [(n_big * BIG, SMALL), (n_big * BIG + SMALL, SMALL)]
-    n_blk = n_big + 2
+    n_blk = len(BLOCKS)
+    blocks = [(sum(BLOCKS[:b]), BLOCKS[b]) for b in range(n_blk)]
     c0 = N_COL * CW
 
     def w_copy(slot, col):
@@ -50,8 +50,8 @@
         cols = pl.ds(j * CW, CW)
         return remote(part.at[k, :, cols], recv.at[k, :, cols], col_tx.at[k, j], col_rx.at[k, j], peers[k])
 
-    def row_copy(k, b, row, n):
-        sl = (k, pl.ds(row, n), pl.ds(c0, d_loc - c0))
+    def row_copy(k, b):
+        sl = (k, pl.ds(*blocks[b]), pl.ds(c0, d_loc - c0))
         return remote(part.at[sl], recv.at[sl], row_tx.at[k, b], row_rx.at[k, b], peers[k])
 
     def sib_copy():
@@ -135,16 +135,12 @@
     def _(i):
         cross(i)
 
-    def send_block(b, row, n):
-        row_copy(0, b, row, n).start()
-        row_copy(1, b, row, n).start()
-
-    def sent_block(b, row, n):
-        row_copy(0, b, row, n).wait_send()
-        row_copy(1, b, row, n).wait_send()
+    def send_block(b):
+        row_copy(0, b).start()
+        row_copy(1, b).start()
 
     for b in range(AHEAD):
-        send_block(b, b * BIG, BIG)
+        send_block(b)
     r_copy.start()
     g_copy.start()
 
@@ -169,63 +165,55 @@
     lane = lax.broadcasted_iota(jnp.int32, (8, 128), 1)
     sub = lax.broadcasted_iota(jnp.int32, (8, 128), 0)
 
-    def reduce_block(b, row, n):
-        row_copy(0, b, row, n).wait_recv()
-        row_copy(1, b, row, n).wait_recv()
-        sl = pl.ds(row, n)
-        h = own[sl, :] + recv[0, sl, :].astype(F32) + recv[1, sl, :].astype(F32) + recv[2, sl, :].astype(F32)
-        h = r_v[sl, :].astype(F32) + h
-        own[sl, :] = h
-        hid[sl, :] = h.astype(BF16)
-        s = jnp.sum(h * h, axis=1, keepdims=True)
+    def reduce_block(b):
+        row_copy(0, b).wait_recv()
+        row_copy(1, b).wait_recv()
+        row, n = blocks[b]
         line = jnp.zeros((8, 128), F32)
-        for q in range(n // 8):
-            line = line + jnp.where(lane == sub + 8 * q, s[8 * q:8 * q + 8, :], 0.0)
+        for first in range(0, n, SUB):
+            sl = pl.ds(row + first, SUB)
+            h = own[sl, :] + recv[0, sl, :].astype(F32) + recv[1, sl, :].astype(F32) + recv[2, sl, :].astype(F32)
+            h = r_v[sl, :].astype(F32) + h
+            own[sl, :] = h
+            hid[sl, :] = h.astype(BF16)
+            s = jnp.sum(h * h, axis=1, keepdims=True)
+            for q in range(0, SUB, 8):
+                line = line + jnp.where(lane == sub + (first + q), s[q:q + 8, :], 0.0)
         st_tx[b] = jnp.sum(line, axis=0, keepdims=True)
         for k in range(3):
             stat_copy(k, b).start()
 
-    def norm_block(b, row, n):
+    def norm_block(b):
         for k in range(3):
             stat_copy(k, b).wait_recv()
+        row, n = blocks[b]
         tot = (st_tx[b] + st_rx[2, b]) + (st_rx[0, b] + st_rx[1, b])
-        scale = lax.rsqrt(tot / d_model + EPS)
-        scale = jnp.broadcast_to(scale, (8, 128))
-        for q in range(n // 8):
-            sl = pl.ds(row + 8 * q, 8)
-            col = jnp.sum(jnp.where(lane == sub + 8 * q, scale, 0.0), axis=1, keepdims=True)
-            own[sl, :] = own[sl, :] * col * g_v[...]
-        sl = pl.ds(row, n)
-        nrm[sl, :] = own[sl, :].astype(BF16)
-
-    (row_s, n_s), (row_l, n_l) = blocks
-
-    sent_block(0, 0, BIG)
-    send_block(AHEAD, AHEAD * BIG, BIG)
-    reduce_block(0, 0, BIG)
-
-    @pl.loop(1, n_big - AHEAD)
-    def _(b):
-        row = pl.multiple_of(b * BIG, BIG)
-        sent_block(b, row, BIG)
-        send_block(b + AHEAD, pl.multiple_of(row + AHEAD * BIG, BIG), BIG)
-        reduce_block(b, row, BIG)
-        norm_block(b - 1, pl.multiple_of(row - BIG, BIG), BIG)
-
-    for q in range(2):
-        b = n_big - 2 + q
-        sent_block(b, b * BIG, BIG)
-        send_block(n_big + q, *blocks[q])
-        reduce_block(b, b * BIG, BIG)
-        norm_block(b - 1, b * BIG - BIG, BIG)
-
-    reduce_block(n_big, row_s, n_s)
-    reduce_block(n_big + 1, row_l, n_l)
-    norm_block(n_big - 1, row_s - BIG, BIG)
-    norm_block(n_big, row_s, n_s)
-    norm_block(n_big + 1, row_l, n_l)
-    sent_block(n_big, row_s, n_s)
-    sent_block(n_big + 1, row_l, n_l)
+        scale = jnp.broadcast_to(lax.rsqrt(tot / d_model + EPS), (8, 128))
+        for first in range(0, n, SUB):
+            for q in range(first, first + SUB, 8):
+                sl = pl.ds(row + q, 8)
+                col = jnp.sum(jnp.where(lane == sub + q, scale, 0.0), axis=1, keepdims=True)
+                own[sl, :] = own[sl, :] * col * g_v[...]
+            sl = pl.ds(row + first, SUB)
+            nrm[sl, :] = own[sl, :].astype(BF16)
+
+    for b in range(n_blk - 2):
+        row_copy(0, b).wait_send()
+        row_copy(1, b).wait_send()
+        if b + AHEAD < n_blk:
+            send_block(b + AHEAD)
+        reduce_block(b)
+        if b:
+            norm_block(b - 1)
+
+    reduce_block(n_blk - 2)
+    reduce_block(n_blk - 1)
+    for b in range(n_blk - 3, n_blk):
+        norm_block(b)
+
+    for b in range(n_blk - 2, n_blk):
+        row_copy(0, b).wait_send()
+        row_copy(1, b).wait_send()
 
     for q in range(len(pieces)):
         piece_copy(q).wait_send()
@@ -233,7 +221,7 @@
         col_copy(i % 2, i // 2).wait_send()
     sib_copy().wait_send()
 
-    @pl.loop(0, n_big + 2)
+    @pl.loop(0, n_blk)
     def _(b):
         for k in range(3):
             stat_copy(k, b).wait_send()
@@ -259,7 +247,7 @@
         rows, depth = a.shape
         d_loc = r.shape[1]
         per = d_loc // CW
-        n_blk = (rows - 2 * SMALL) // BIG + 2
+        n_blk = len(BLOCKS)
         hbm = pl.BlockSpec(memory_space=pltpu.HBM)
         vmem = pl.BlockSpec(memory_space=pltpu.VMEM)
         dma = pltpu.SemaphoreType.DMA

time: 57.4 us -> 57 us (level)
  no operation moved by 1% of the time
where the time goes in v6:
time: 57 us; the launch traced here: 56.8 us
  Pallas kernels  56.2 us (99%)
  between operations  0.64 us (1%)
    pallas_call x1, Pallas kernels, local_step(): pl.pallas_call(functools.partial(kernel, d_loc * tp), out_shape=(pltpu.VM...  54.9 us
    pallas_call x1, Pallas kernels, local_step(): pl.pallas_call(put, out_shape=(jax.ShapeDtypeStruct((rows, d_loc), BF16),...  1.33 us

profile of v6, /device:TPU:0, one launch (start us, length us, event | category | flops | bytes accessed | tf_op | source)
XLA Modules:
  0.0 56.8 jit_solution(2472600986063031198)
XLA Ops:
  0.6 54.9 %shard_map.59 = (bf16[256,2048]{1,0:T(8,128)(2,1)S(1)}, bf16[256,2048]{1,0:T(8,128)(2,1)S(1)}) custom-call(bf16[256,2048]{1,0:T(8,128)(2,1)} %a_hbm.1, bf16[2048,8192]{1,0:T(8,128)(2,1)} %w_hbm.1, bf16[256,2048]{1,0:T(8,128)(2,1)} %r_hbm.1, f32[1,2048]{1,0:T(1,128)} %bitcast.1), custom_call_target="tpu_custom_call" | custom-call | flops 8589934592 | bytes 33554432 | tf_op jit(solution)/shard_map/pallas_call | solution.py:254
  55.5 1.3 %shard_map.60 = (bf16[256,2048]{1,0:T(8,128)(2,1)}, bf16[256,2048]{1,0:T(8,128)(2,1)}) custom-call(bf16[256,2048]{1,0:T(8,128)(2,1)S(1)} %get-tuple-element.4.hid, bf16[256,2048]{1,0:T(8,128)(2,1)S(1)} %get-tuple-element.5.nrm), custom_call_target="tpu_custom_call" | custom-call | tf_op jit(solution)/shard_map/pallas_call | solution.py:278

commit v7 on v6

--- a/solution.py
+++ b/solution.py
@@ -17,6 +17,7 @@
 SUB = 16
 DEPTH = 4
 PUT = 1
+LAG = 2
 AHEAD = 2
 
 
@@ -203,12 +204,12 @@
         if b + AHEAD < n_blk:
             send_block(b + AHEAD)
         reduce_block(b)
-        if b:
-            norm_block(b - 1)
+        if b >= LAG:
+            norm_block(b - LAG)
 
     reduce_block(n_blk - 2)
     reduce_block(n_blk - 1)
-    for b in range(n_blk - 3, n_blk):
+    for b in range(n_blk - 2 - LAG, n_blk):
         norm_block(b)
 
     for b in range(n_blk - 2, n_blk):

time: 57 us -> 56 us (0.982)
  Pallas kernels: 56.2 us -> 55.2 us
    pallas_call x1, Pallas kernels: 54.9 us -> 53.9 us  [local_step(): pl.pallas_call(functools.partial(kernel, d_loc * tp), out_shape=(pltpu.VM...]
where the time goes in v7:
time: 56 us; the launch traced here: 55.9 us
  Pallas kernels  55.2 us (99%)
  between operations  0.64 us (1%)
    pallas_call x1, Pallas kernels, local_step(): pl.pallas_call(functools.partial(kernel, d_loc * tp), out_shape=(pltpu.VM...  53.9 us
    pallas_call x1, Pallas kernels, local_step(): pl.pallas_call(put, out_shape=(jax.ShapeDtypeStruct((rows, d_loc), BF16),...  1.33 us

profile of v7, /device:TPU:0, one launch (start us, length us, event | category | flops | bytes accessed | tf_op | source)
XLA Modules:
  0.0 55.9 jit_solution(17658256015095473062)
XLA Ops:
  0.6 53.9 %shard_map.59 = (bf16[256,2048]{1,0:T(8,128)(2,1)S(1)}, bf16[256,2048]{1,0:T(8,128)(2,1)S(1)}) custom-call(bf16[256,2048]{1,0:T(8,128)(2,1)} %a_hbm.1, bf16[2048,8192]{1,0:T(8,128)(2,1)} %w_hbm.1, bf16[256,2048]{1,0:T(8,128)(2,1)} %r_hbm.1, f32[1,2048]{1,0:T(1,128)} %bitcast.1), custom_call_target="tpu_custom_call" | custom-call | flops 8589934592 | bytes 33554432 | tf_op jit(solution)/shard_map/pallas_call | solution.py:255
  54.5 1.3 %shard_map.60 = (bf16[256,2048]{1,0:T(8,128)(2,1)}, bf16[256,2048]{1,0:T(8,128)(2,1)}) custom-call(bf16[256,2048]{1,0:T(8,128)(2,1)S(1)} %get-tuple-element.4.hid, bf16[256,2048]{1,0:T(8,128)(2,1)S(1)} %get-tuple-element.5.nrm), custom_call_target="tpu_custom_call" | custom-call | tf_op jit(solution)/shard_map/pallas_call | solution.py:279

commit v8 on v6

--- a/solution.py
+++ b/solution.py
@@ -13,7 +13,7 @@
 
 CW = 256
 N_COL = 2
-BLOCKS = (64, 64, 64, 32, 16, 16)
+BLOCKS = (128, 112, 16)
 SUB = 16
 DEPTH = 4
 PUT = 1
@@ -52,7 +52,8 @@
 
     def row_copy(k, b):
         sl = (k, pl.ds(*blocks[b]), pl.ds(c0, d_loc - c0))
-        return remote(part.at[sl], recv.at[sl], row_tx.at[k, b], row_rx.at[k, b], peers[k])
+        return remote(part.at[sl], recv.at[sl], row_tx.at[k, b], row_rx.at[k, b],
+                      peers[0] + (peers[1] - peers[0]) * k)
 
     def sib_copy():
         return remote(part.at[2], recv.at[2], sib_tx, sib_rx, peers[2])
@@ -136,8 +137,8 @@
         cross(i)
 
     def send_block(b):
-        row_copy(0, b).start()
-        row_copy(1, b).start()
+        row_copy(t % 2, b).start()
+        row_copy(1 - t % 2, b).start()
 
     for b in range(AHEAD):
         send_block(b)
@@ -197,29 +198,25 @@
             sl = pl.ds(row + first, SUB)
             nrm[sl, :] = own[sl, :].astype(BF16)
 
-    for b in range(n_blk - 2):
-        row_copy(0, b).wait_send()
-        row_copy(1, b).wait_send()
+    for b in range(n_blk):
         if b + AHEAD < n_blk:
+            row_copy(0, b).wait_send()
+            row_copy(1, b).wait_send()
             send_block(b + AHEAD)
         reduce_block(b)
-        if b:
-            norm_block(b - 1)
-
-    reduce_block(n_blk - 2)
-    reduce_block(n_blk - 1)
-    for b in range(n_blk - 3, n_blk):
+
+    for b in range(n_blk):
         norm_block(b)
-
-    for b in range(n_blk - 2, n_blk):
-        row_copy(0, b).wait_send()
-        row_copy(1, b).wait_send()
 
     for q in range(len(pieces)):
         piece_copy(q).wait_send()
     for i in range(1, 2 * N_COL):
         col_copy(i % 2, i // 2).wait_send()
     sib_copy().wait_send()
+
+    for b in range(n_blk - AHEAD, n_blk):
+        row_copy(0, b).wait_send()
+        row_copy(1, b).wait_send()
 
     @pl.loop(0, n_blk)
     def _(b):

time: 57 us -> 55.4 us (0.972)
  Pallas kernels: 56.2 us -> 54.6 us
    pallas_call x1, Pallas kernels: 54.9 us -> 53.3 us  [local_step(): pl.pallas_call(functools.partial(kernel, d_loc * tp), out_shape=(pltpu.VM...]
where the time goes in v8:
time: 55.4 us; the launch traced here: 55.2 us
  Pallas kernels  54.6 us (99%)
  between operations  0.64 us (1%)
    pallas_call x1, Pallas kernels, local_step(): pl.pallas_call(functools.partial(kernel, d_loc * tp), out_shape=(pltpu.VM...  53.3 us
    pallas_call x1, Pallas kernels, local_step(): pl.pallas_call(put, out_shape=(jax.ShapeDtypeStruct((rows, d_loc), BF16),...  1.33 us

profile of v8, /device:TPU:0, one launch (start us, length us, event | category | flops | bytes accessed | tf_op | source)
XLA Modules:
  0.0 55.2 jit_solution(5098184979800420343)
XLA Ops:
  0.6 53.3 %shard_map.59 = (bf16[256,2048]{1,0:T(8,128)(2,1)S(1)}, bf16[256,2048]{1,0:T(8,128)(2,1)S(1)}) custom-call(bf16[256,2048]{1,0:T(8,128)(2,1)} %a_hbm.1, bf16[2048,8192]{1,0:T(8,128)(2,1)} %w_hbm.1, bf16[256,2048]{1,0:T(8,128)(2,1)} %r_hbm.1, f32[1,2048]{1,0:T(1,128)} %bitcast.1), custom_call_target="tpu_custom_call" | custom-call | flops 8589934592 | bytes 33554432 | tf_op jit(solution)/shard_map/pallas_call | solution.py:251
  53.9 1.3 %shard_map.60 = (bf16[256,2048]{1,0:T(8,128)(2,1)}, bf16[256,2048]{1,0:T(8,128)(2,1)}) custom-call(bf16[256,2048]{1,0:T(8,128)(2,1)S(1)} %get-tuple-element.4.hid, bf16[256,2048]{1,0:T(8,128)(2,1)S(1)} %get-tuple-element.5.nrm), custom_call_target="tpu_custom_call" | custom-call | tf_op jit(solution)/shard_map/pallas_call | solution.py:275

commit v9 on v8

--- a/solution.py
+++ b/solution.py
@@ -17,7 +17,7 @@
 SUB = 16
 DEPTH = 4
 PUT = 1
-AHEAD = 2
+AHEAD = 3
 
 
 def kernel(d_model, a_hbm, w_hbm, r_hbm, g_hbm, hid, nrm,

time: 55.4 us -> 55.4 us (level)
  no operation moved by 1% of the time
where the time goes in v9:
time: 55.4 us; the launch traced here: 55.2 us
  Pallas kernels  54.6 us (99%)
  between operations  0.64 us (1%)
    pallas_call x1, Pallas kernels, local_step(): pl.pallas_call(functools.partial(kernel, d_loc * tp), out_shape=(pltpu.VM...  53.3 us
    pallas_call x1, Pallas kernels, local_step(): pl.pallas_call(put, out_shape=(jax.ShapeDtypeStruct((rows, d_loc), BF16),...  1.33 us

profile of v9, /device:TPU:0, one launch (start us, length us, event | category | flops | bytes accessed | tf_op | source)
XLA Modules:
  0.0 55.2 jit_solution(17280276252086336463)
XLA Ops:
  0.6 53.3 %shard_map.59 = (bf16[256,2048]{1,0:T(8,128)(2,1)S(1)}, bf16[256,2048]{1,0:T(8,128)(2,1)S(1)}) custom-call(bf16[256,2048]{1,0:T(8,128)(2,1)} %a_hbm.1, bf16[2048,8192]{1,0:T(8,128)(2,1)} %w_hbm.1, bf16[256,2048]{1,0:T(8,128)(2,1)} %r_hbm.1, f32[1,2048]{1,0:T(1,128)} %bitcast.1), custom_call_target="tpu_custom_call" | custom-call | flops 8589934592 | bytes 33554432 | tf_op jit(solution)/shard_map/pallas_call | solution.py:251
  53.9 1.3 %shard_map.60 = (bf16[256,2048]{1,0:T(8,128)(2,1)}, bf16[256,2048]{1,0:T(8,128)(2,1)}) custom-call(bf16[256,2048]{1,0:T(8,128)(2,1)S(1)} %get-tuple-element.4.hid, bf16[256,2048]{1,0:T(8,128)(2,1)S(1)} %get-tuple-element.5.nrm), custom_call_target="tpu_custom_call" | custom-call | tf_op jit(solution)/shard_map/pallas_call | solution.py:275

commit v10 on v9

--- a/solution.py
+++ b/solution.py
@@ -17,7 +17,6 @@
 SUB = 16
 DEPTH = 4
 PUT = 1
-AHEAD = 3
 
 
 def kernel(d_model, a_hbm, w_hbm, r_hbm, g_hbm, hid, nrm,
@@ -118,6 +117,15 @@
         part[0, r_sl, c_sl] = dot(a_v[r_sl, :], w_v[0, :, c_sl]).astype(BF16)
         if q == 0:
             pl.semaphore_wait(barrier, 3)
+        if q == 1:
+            @pl.when(t % 2 == 0)
+            def _():
+                piece_copy(1).start()
+            continue
+        if q == 2:
+            @pl.when(t % 2 == 1)
+            def _():
+                piece_copy(1).start()
         piece_copy(q).start()
 
     def chunk(i, col):
@@ -136,12 +144,11 @@
     def _(i):
         cross(i)
 
-    def send_block(b):
-        row_copy(t % 2, b).start()
-        row_copy(1 - t % 2, b).start()
-
-    for b in range(AHEAD):
-        send_block(b)
+    far, near = t % 2, 1 - t % 2
+    order = ([(k, b) for b in range(n_blk - 2) for k in (far, near)]
+             + [(k, b) for k in (far, near) for b in (n_blk - 2, n_blk - 1)])
+    for k, b in order:
+        row_copy(k, b).start()
     r_copy.start()
     g_copy.start()
 
@@ -199,10 +206,6 @@
             nrm[sl, :] = own[sl, :].astype(BF16)
 
     for b in range(n_blk):
-        if b + AHEAD < n_blk:
-            row_copy(0, b).wait_send()
-            row_copy(1, b).wait_send()
-            send_block(b + AHEAD)
         reduce_block(b)
 
     for b in range(n_blk):
@@ -214,7 +217,7 @@
         col_copy(i % 2, i // 2).wait_send()
     sib_copy().wait_send()
 
-    for b in range(n_blk - AHEAD, n_blk):
+    for b in range(n_blk):
         row_copy(0, b).wait_send()
         row_copy(1, b).wait_send()
 

time: 55.4 us -> 55.7 us (level)
  no operation moved by 1% of the time
where the time goes in v10:
time: 55.7 us; the launch traced here: 55.6 us
  Pallas kernels  54.9 us (99%)
  between operations  0.64 us (1%)
    pallas_call x1, Pallas kernels, local_step(): pl.pallas_call(functools.partial(kernel, d_loc * tp), out_shape=(pltpu.VM...  53.6 us
    pallas_call x1, Pallas kernels, local_step(): pl.pallas_call(put, out_shape=(jax.ShapeDtypeStruct((rows, d_loc), BF16),...  1.33 us

profile of v10, /device:TPU:0, one launch (start us, length us, event | category | flops | bytes accessed | tf_op | source)
XLA Modules:
  0.0 55.6 jit_solution(5407524709371660651)
XLA Ops:
  0.6 53.6 %shard_map.59 = (bf16[256,2048]{1,0:T(8,128)(2,1)S(1)}, bf16[256,2048]{1,0:T(8,128)(2,1)S(1)}) custom-call(bf16[256,2048]{1,0:T(8,128)(2,1)} %a_hbm.1, bf16[2048,8192]{1,0:T(8,128)(2,1)} %w_hbm.1, bf16[256,2048]{1,0:T(8,128)(2,1)} %r_hbm.1, f32[1,2048]{1,0:T(1,128)} %bitcast.1), custom_call_target="tpu_custom_call" | custom-call | flops 8589934592 | bytes 33554432 | tf_op jit(solution)/shard_map/pallas_call | solution.py:254
  54.2 1.3 %shard_map.60 = (bf16[256,2048]{1,0:T(8,128)(2,1)}, bf16[256,2048]{1,0:T(8,128)(2,1)}) custom-call(bf16[256,2048]{1,0:T(8,128)(2,1)S(1)} %get-tuple-element.4.hid, bf16[256,2048]{1,0:T(8,128)(2,1)S(1)} %get-tuple-element.5.nrm), custom_call_target="tpu_custom_call" | custom-call | tf_op jit(solution)/shard_map/pallas_call | solution.py:278

commit v11 on v10

--- a/solution.py
+++ b/solution.py
@@ -117,15 +117,6 @@
         part[0, r_sl, c_sl] = dot(a_v[r_sl, :], w_v[0, :, c_sl]).astype(BF16)
         if q == 0:
             pl.semaphore_wait(barrier, 3)
-        if q == 1:
-            @pl.when(t % 2 == 0)
-            def _():
-                piece_copy(1).start()
-            continue
-        if q == 2:
-            @pl.when(t % 2 == 1)
-            def _():
-                piece_copy(1).start()
         piece_copy(q).start()
 
     def chunk(i, col):
@@ -145,8 +136,7 @@
         cross(i)
 
     far, near = t % 2, 1 - t % 2
-    order = ([(k, b) for b in range(n_blk - 2) for k in (far, near)]
-             + [(k, b) for k in (far, near) for b in (n_blk - 2, n_blk - 1)])
+    order = [(k, b) for b in range(n_blk) for k in (near, far)]
     for k, b in order:
         row_copy(k, b).start()
     r_copy.start()

time: 55.7 us -> 56 us (level)
  no operation moved by 1% of the time
where the time goes in v11:
time: 56 us; the launch traced here: 55.9 us
  Pallas kernels  55.3 us (99%)
  between operations  0.64 us (1%)
    pallas_call x1, Pallas kernels, local_step(): pl.pallas_call(functools.partial(kernel, d_loc * tp), out_shape=(pltpu.VM...  53.9 us
    pallas_call x1, Pallas kernels, local_step(): pl.pallas_call(put, out_shape=(jax.ShapeDtypeStruct((rows, d_loc), BF16),...  1.33 us

profile of v11, /device:TPU:0, one launch (start us, length us, event | category | flops | bytes accessed | tf_op | source)
XLA Modules:
  0.0 55.9 jit_solution(10044661471569350580)
XLA Ops:
  0.6 53.9 %shard_map.59 = (bf16[256,2048]{1,0:T(8,128)(2,1)S(1)}, bf16[256,2048]{1,0:T(8,128)(2,1)S(1)}) custom-call(bf16[256,2048]{1,0:T(8,128)(2,1)} %a_hbm.1, bf16[2048,8192]{1,0:T(8,128)(2,1)} %w_hbm.1, bf16[256,2048]{1,0:T(8,128)(2,1)} %r_hbm.1, f32[1,2048]{1,0:T(1,128)} %bitcast.1), custom_call_target="tpu_custom_call" | custom-call | flops 8589934592 | bytes 33554432 | tf_op jit(solution)/shard_map/pallas_call | solution.py:244
  54.6 1.3 %shard_map.60 = (bf16[256,2048]{1,0:T(8,128)(2,1)}, bf16[256,2048]{1,0:T(8,128)(2,1)}) custom-call(bf16[256,2048]{1,0:T(8,128)(2,1)S(1)} %get-tuple-element.4.hid, bf16[256,2048]{1,0:T(8,128)(2,1)S(1)} %get-tuple-element.5.nrm), custom_call_target="tpu_custom_call" | custom-call | tf_op jit(solution)/shard_map/pallas_call | solution.py:268

commit v12 on v11

--- a/solution.py
+++ b/solution.py
@@ -136,7 +136,8 @@
         cross(i)
 
     far, near = t % 2, 1 - t % 2
-    order = [(k, b) for b in range(n_blk) for k in (near, far)]
+    order = ([(k, b) for b in range(n_blk - 2) for k in (far, near)]
+             + [(k, b) for k in (far, near) for b in (n_blk - 2, n_blk - 1)])
     for k, b in order:
         row_copy(k, b).start()
     r_copy.start()

time: 56 us -> 55.1 us (0.984)
  Pallas kernels: 55.3 us -> 54.4 us
    pallas_call x1, Pallas kernels: 53.9 us -> 53.1 us  [local_step(): pl.pallas_call(functools.partial(kernel, d_loc * tp), out_shape=(pltpu.VM...]
where the time goes in v12:
time: 55.1 us; the launch traced here: 55 us
  Pallas kernels  54.4 us (99%)
  between operations  0.64 us (1%)
    pallas_call x1, Pallas kernels, local_step(): pl.pallas_call(functools.partial(kernel, d_loc * tp), out_shape=(pltpu.VM...  53.1 us
    pallas_call x1, Pallas kernels, local_step(): pl.pallas_call(put, out_shape=(jax.ShapeDtypeStruct((rows, d_loc), BF16),...  1.33 us

profile of v12, /device:TPU:0, one launch (start us, length us, event | category | flops | bytes accessed | tf_op | source)
XLA Modules:
  0.0 55.0 jit_solution(18012584347687248797)
XLA Ops:
  0.6 53.1 %shard_map.59 = (bf16[256,2048]{1,0:T(8,128)(2,1)S(1)}, bf16[256,2048]{1,0:T(8,128)(2,1)S(1)}) custom-call(bf16[256,2048]{1,0:T(8,128)(2,1)} %a_hbm.1, bf16[2048,8192]{1,0:T(8,128)(2,1)} %w_hbm.1, bf16[256,2048]{1,0:T(8,128)(2,1)} %r_hbm.1, f32[1,2048]{1,0:T(1,128)} %bitcast.1), custom_call_target="tpu_custom_call" | custom-call | flops 8589934592 | bytes 33554432 | tf_op jit(solution)/shard_map/pallas_call | solution.py:245
  53.7 1.3 %shard_map.60 = (bf16[256,2048]{1,0:T(8,128)(2,1)}, bf16[256,2048]{1,0:T(8,128)(2,1)}) custom-call(bf16[256,2048]{1,0:T(8,128)(2,1)S(1)} %get-tuple-element.4.hid, bf16[256,2048]{1,0:T(8,128)(2,1)S(1)} %get-tuple-element.5.nrm), custom_call_target="tpu_custom_call" | custom-call | tf_op jit(solution)/shard_map/pallas_call | solution.py:269

commit v13 on v11

v13 whole, which is shorter than its diff:
```python
import functools

import jax
import jax.numpy as jnp
from jax import lax
from jax.experimental import pallas as pl
from jax.experimental.pallas import tpu as pltpu
from jax.sharding import PartitionSpec as P

EPS = 1e-5
MESH = pl.DeviceIdType.MESH
F32, BF16 = jnp.float32, jnp.bfloat16

CW = 256
N_COL = 2
BLOCKS = (128, 112, 16)
SUB = 16
DEPTH = 4
PUT = 1
FAR, NEAR, SIB = 0, 1, 2


def kernel(d_model, a_hbm, w_hbm, r_hbm, g_hbm, hid, nrm,
           a_v, w_v, r_v, g_v, part, recv, own, st_tx, st_rx,
           a_sem, w0_sem, w_sem, r_sem, g_sem, far_tx, far_rx, near_tx, near_rx, sib_tx, sib_rx, stat_tx, stat_rx):
    t = lax.axis_index("tp")
    core, chip = t % 2, t // 2
    rows, _ = a_v.shape
    d_loc = own.shape[1]
    per = d_loc // CW
    n_blk = len(BLOCKS)
    blocks = [(sum(BLOCKS[:b]), BLOCKS[b]) for b in range(n_blk)]
    half, lanes = rows // 2, 128
    far, near, sib = 2 - 2 * chip, 3 - 2 * chip, t + 1 - 2 * core

    def cross_col(i):
        return (far + i // per) * d_loc + (i % per) * CW

    def home_col(i):
        return (sib + (t - sib) * (i // per)) * d_loc + (i % per) * CW

    def w_copy(i, col):
        return pltpu.make_async_copy(w_hbm.at[:, pl.ds(pl.multiple_of(col, CW), CW)], w_v.at[i], w_sem.at[i])

    def w_start(i):
        if isinstance(i, int):
            w_copy(i, cross_col(i) if i < 2 * per else home_col(i - 2 * per)).start()
            return

        @pl.when(i < 2 * per)
        def _():
            w_copy(i, cross_col(i)).start()

        @pl.when((i >= 2 * per) & (i < 4 * per))
        def _():
            w_copy(i, home_col(i - 2 * per)).start()

    def a_copy(q):
        sl = pl.ds(q * half, half)
        return pltpu.make_async_copy(a_hbm.at[sl, :], a_v.at[sl, :], a_sem.at[q])

    def w0_copy(q):
        src = w_hbm.at[:, pl.ds(pl.multiple_of(far * d_loc + q * lanes, lanes), lanes)]
        return pltpu.make_async_copy(src, w_v.at[0, :, pl.ds(q * lanes, lanes)], w0_sem.at[q])

    def remote(src, dst, tx, rx, peer):
        return pltpu.make_async_remote_copy(src_ref=src, dst_ref=dst, send_sem=tx, recv_sem=rx,
                                            device_id={"tp": peer}, device_id_type=MESH)

    every = pl.ds(0, rows)
    far_parts = [(pl.ds(0, half), pl.ds(0, lanes)), (pl.ds(0, half), pl.ds(lanes, lanes)), (pl.ds(half, half), pl.ds(0, CW))]
    far_parts += [(every, pl.ds(j * CW, CW)) for j in range(1, N_COL)]
    far_parts += [(every, pl.ds(N_COL * CW, d_loc - N_COL * CW))]

    def far_copy(q, slot):
        sl = far_parts[q]
        return remote(part.at[(FAR, *sl)], recv.at[(slot, *sl)], far_tx.at[q], far_rx.at[slot, q], far)

    def near_copy(b, slot):
        sl = pl.ds(*blocks[b])
        return remote(part.at[NEAR, sl, :], recv.at[slot, sl, :], near_tx.at[b], near_rx.at[slot, b], near)

    def sib_copy():
        return remote(part.at[SIB], recv.at[SIB], sib_tx, sib_rx, sib)

    def stat_copy(k, b, slot):
        return remote(st_tx.at[b], st_rx.at[slot, b], stat_tx.at[k, b], stat_rx.at[slot, b], (far, near, sib)[k])

    a_copy(0).start()
    w0_copy(0).start()
    w0_copy(1).start()
    a_copy(1).start()
    r_copy = pltpu.make_async_copy(r_hbm, r_v, r_sem)
    g_copy = pltpu.make_async_copy(g_hbm, g_v, g_sem)
    barrier = pltpu.get_barrier_semaphore()
    for p in (far, near, sib):
        pl.semaphore_signal(barrier, inc=1, device_id={"tp": p}, device_id_type=MESH)

    def dot(lhs, rhs):
        return jnp.dot(lhs, rhs, preferred_element_type=F32)

    for q in range(3):
        if q == 0:
            a_copy(0).wait()
            w0_copy(0).wait()
            for i in range(1, DEPTH):
                w_start(i)
        elif q == 1:
            w0_copy(1).wait()
        else:
            a_copy(1).wait()
            w_start(DEPTH)
        r_sl, c_sl = far_parts[q]
        part[FAR, r_sl, c_sl] = dot(a_v[r_sl, :], w_v[0, :, c_sl]).astype(BF16)
        if q == 0:
            pl.semaphore_wait(barrier, 3)
        far_copy(q, core).start()

    def chunk(i, col):
        w_copy(i, col).wait()
        w_start(i + DEPTH)
        return dot(a_v[...], w_v[i])

    def columns(j):
        return pl.ds(pl.multiple_of(j * CW, CW), CW)

    for j in range(1, N_COL):
        part[FAR, :, columns(j)] = chunk(j, cross_col(j)).astype(BF16)
        far_copy(2 + j, core).start()

    @pl.loop(N_COL, per)
    def _(j):
        part[FAR, :, columns(j)] = chunk(j, cross_col(j)).astype(BF16)

    far_copy(len(far_parts) - 1, core).start()

    @pl.loop(0, per)
    def _(j):
        part[NEAR, :, columns(j)] = chunk(per + j, cross_col(per + j)).astype(BF16)

    for b in range(n_blk):
        near_copy(b, core).start()
    r_copy.start()
    g_copy.start()

    @pl.loop(0, per)
    def _(j):
        part[SIB, :, columns(j)] = chunk(2 * per + j, home_col(j)).astype(BF16)

    sib_copy().start()

    @pl.loop(0, per)
    def _(j):
        own[:, columns(j)] = chunk(3 * per + j, home_col(per + j))

    r_copy.wait()
    g_copy.wait()
    sib_copy().wait_recv()

    @pl.when(core == 0)
    def _():
        for q in range(len(far_parts)):
            for slot in range(2):
                far_copy(q, slot).wait_recv()

    lane = lax.broadcasted_iota(jnp.int32, (8, 128), 1)
    sub = lax.broadcasted_iota(jnp.int32, (8, 128), 0)

    def reduce_block(b):
        @pl.when(core == 1)
        def _():
            for slot in range(2):
                near_copy(b, slot).wait_recv()

        row, n = blocks[b]
        line = jnp.zeros((8, 128), F32)
        for first in range(0, n, SUB):
            sl = pl.ds(row + first, SUB)
            h = own[sl, :] + recv[SIB, sl, :].astype(F32) + recv[0, sl, :].astype(F32) + recv[1, sl, :].astype(F32)
            h = r_v[sl, :].astype(F32) + h
            own[sl, :] = h
            hid[sl, :] = h.astype(BF16)
            s = jnp.sum(h * h, axis=1, keepdims=True)
            for q in range(0, SUB, 8):
                line = line + jnp.where(lane == sub + (first + q), s[q:q + 8, :], 0.0)
        st_tx[b] = jnp.sum(line, axis=0, keepdims=True)
        for k in range(3):
            stat_copy(k, b, SIB if k == SIB else core).start()

    def norm_block(b):
        for slot in range(3):
            stat_copy(slot, b, slot).wait_recv()
        row, n = blocks[b]
        tot = (st_tx[b] + st_rx[SIB, b]) + (st_rx[0, b] + st_rx[1, b])
        scale = jnp.broadcast_to(lax.rsqrt(tot / d_model + EPS), (8, 128))
        for first in range(0, n, SUB):
            for q in range(first, first + SUB, 8):
                sl = pl.ds(row + q, 8)
                col = jnp.sum(jnp.where(lane == sub + q, scale, 0.0), axis=1, keepdims=True)
                own[sl, :] = own[sl, :] * col * g_v[...]
            sl = pl.ds(row + first, SUB)
            nrm[sl, :] = own[sl, :].astype(BF16)

    for b in range(n_blk):
        reduce_block(b)

    for b in range(n_blk):
        norm_block(b)

    for q in range(len(far_parts)):
        far_copy(q, core).wait_send()
    for b in range(n_blk):
        near_copy(b, core).wait_send()
        for k in range(3):
            stat_copy(k, b, SIB if k == SIB else core).wait_send()
    sib_copy().wait_send()


def put(hid, nrm, hid_hbm, nrm_hbm, sem):
    n = hid.shape[0] // PUT
    copies = []
    for q in range(PUT):
        sl = pl.ds(q * n, n)
        copies.append(pltpu.make_async_copy(hid.at[sl, :], hid_hbm.at[sl, :], sem.at[0, q]))
        copies.append(pltpu.make_async_copy(nrm.at[sl, :], nrm_hbm.at[sl, :], sem.at[1, q]))
    for c in copies:
        c.start()
    for c in copies:
        c.wait()


def solution(mesh):
    tp = mesh.shape["tp"]

    def local_step(a, w, r, g):
        rows, depth = a.shape
        d_loc = r.shape[1]
        per = d_loc // CW
        n_blk = len(BLOCKS)
        hbm = pl.BlockSpec(memory_space=pltpu.HBM)
        vmem = pl.BlockSpec(memory_space=pltpu.VMEM)
        dma = pltpu.SemaphoreType.DMA
        hid, nrm = pl.pallas_call(
            functools.partial(kernel, d_loc * tp),
            out_shape=(pltpu.VMEM((rows, d_loc), BF16),) * 2,
            in_specs=[hbm] * 4,
            out_specs=(vmem,) * 2,
            scratch_shapes=[
                pltpu.VMEM((rows, depth), BF16),
                pltpu.VMEM((4 * per, depth, CW), BF16),
                pltpu.VMEM((rows, d_loc), BF16),
                pltpu.VMEM((1, d_loc), F32),
                pltpu.VMEM((3, rows, d_loc), BF16),
                pltpu.VMEM((3, rows, d_loc), BF16),
                pltpu.VMEM((rows, d_loc), F32),
                pltpu.VMEM((n_blk, 1, 128), F32),
                pltpu.VMEM((3, n_blk, 1, 128), F32),
                dma((2,)), dma((2,)), dma((4 * per,)), dma, dma,
                dma((N_COL + 3,)), dma((2, N_COL + 3)), dma((n_blk,)), dma((2, n_blk)), dma, dma,
                dma((3, n_blk)), dma((3, n_blk)),
            ],
            compiler_params=pltpu.CompilerParams(
                collective_id=0, has_side_effects=True, vmem_limit_bytes=64946176),
            cost_estimate=pl.CostEstimate(flops=2 * rows * depth * d_loc * tp, transcendentals=0,
                                          bytes_accessed=2 * depth * d_loc * tp),
        )(a, w, r, g.reshape(1, d_loc))
        return pl.pallas_call(
            put,
            out_shape=(jax.ShapeDtypeStruct((rows, d_loc), BF16),) * 2,
            in_specs=[vmem] * 2,
            out_specs=(hbm,) * 2,
            scratch_shapes=[dma((2, PUT))],
            compiler_params=pltpu.CompilerParams(vmem_limit_bytes=1024 * 1024),
        )(hid, nrm)

    return jax.shard_map(
        local_step,
        mesh=mesh,
        in_specs=(P("data", "tp"), P("tp", None), P("data", "tp"), P("tp")),
        out_specs=(P("data", "tp"), P("data", "tp")),
        check_vma=False,
    )
```

time: 56 us -> 55.1 us (0.984)
  Pallas kernels: 55.3 us -> 54.4 us
    pallas_call x1, Pallas kernels: 53.9 us -> 53 us  [local_step(): pl.pallas_call(functools.partial(kernel, d_loc * tp), out_shape=(pltpu.VM...]
where the time goes in v13:
time: 55.1 us; the launch traced here: 55 us
  Pallas kernels  54.4 us (99%)
  between operations  0.64 us (1%)
    pallas_call x1, Pallas kernels, local_step(): pl.pallas_call(functools.partial(kernel, d_loc * tp), out_shape=(pltpu.VM...  53 us
    pallas_call x1, Pallas kernels, local_step(): pl.pallas_call(put, out_shape=(jax.ShapeDtypeStruct((rows, d_loc), BF16),...  1.33 us

profile of v13, /device:TPU:0, one launch (start us, length us, event | category | flops | bytes accessed | tf_op | source)
XLA Modules:
  0.0 55.0 jit_solution(7697893994343406504)
XLA Ops:
  0.6 53.0 %shard_map.59 = (bf16[256,2048]{1,0:T(8,128)(2,1)S(1)}, bf16[256,2048]{1,0:T(8,128)(2,1)S(1)}) custom-call(bf16[256,2048]{1,0:T(8,128)(2,1)} %a_hbm.1, bf16[2048,8192]{1,0:T(8,128)(2,1)} %w_hbm.1, bf16[256,2048]{1,0:T(8,128)(2,1)} %r_hbm.1, f32[1,2048]{1,0:T(1,128)} %bitcast.1), custom_call_target="tpu_custom_call" | custom-call | flops 8589934592 | bytes 33554432 | tf_op jit(solution)/shard_map/pallas_call | solution.py:243
  53.7 1.3 %shard_map.60 = (bf16[256,2048]{1,0:T(8,128)(2,1)}, bf16[256,2048]{1,0:T(8,128)(2,1)}) custom-call(bf16[256,2048]{1,0:T(8,128)(2,1)S(1)} %get-tuple-element.4.hid, bf16[256,2048]{1,0:T(8,128)(2,1)S(1)} %get-tuple-element.5.nrm), custom_call_target="tpu_custom_call" | custom-call | tf_op jit(solution)/shard_map/pallas_call | solution.py:267

commit v14 on v13

--- a/solution.py
+++ b/solution.py
@@ -138,8 +138,13 @@
     def _(j):
         part[NEAR, :, columns(j)] = chunk(per + j, cross_col(per + j)).astype(BF16)
 
-    for b in range(n_blk):
-        near_copy(b, core).start()
+    near_copy(0, core).start()
+
+    @pl.when(core == 0)
+    def _():
+        for b in range(1, n_blk):
+            near_copy(b, core).start()
+
     r_copy.start()
     g_copy.start()
 
@@ -162,6 +167,12 @@
         for q in range(len(far_parts)):
             for slot in range(2):
                 far_copy(q, slot).wait_recv()
+
+    @pl.when(core == 1)
+    def _():
+        near_copy(0, core).wait_send()
+        for b in range(1, n_blk):
+            near_copy(b, core).start()
 
     lane = lax.broadcasted_iota(jnp.int32, (8, 128), 1)
     sub = lax.broadcasted_iota(jnp.int32, (8, 128), 0)
@@ -209,8 +220,13 @@
 
     for q in range(len(far_parts)):
         far_copy(q, core).wait_send()
+    @pl.when(core == 0)
+    def _():
+        near_copy(0, core).wait_send()
+
     for b in range(n_blk):
-        near_copy(b, core).wait_send()
+        if b:
+            near_copy(b, core).wait_send()
         for k in range(3):
             stat_copy(k, b, SIB if k == SIB else core).wait_send()
     sib_copy().wait_send()

time: 55.1 us -> 55.3 us (level)
  no operation moved by 1% of the time
where the time goes in v14:
time: 55.3 us; the launch traced here: 55.2 us
  Pallas kernels  54.6 us (99%)
  between operations  0.64 us (1%)
    pallas_call x1, Pallas kernels, local_step(): pl.pallas_call(functools.partial(kernel, d_loc * tp), out_shape=(pltpu.VM...  53.2 us
    pallas_call x1, Pallas kernels, local_step(): pl.pallas_call(put, out_shape=(jax.ShapeDtypeStruct((rows, d_loc), BF16),...  1.33 us

profile of v14, /device:TPU:0, one launch (start us, length us, event | category | flops | bytes accessed | tf_op | source)
XLA Modules:
  0.0 55.2 jit_solution(7370545348933856568)
XLA Ops:
  0.6 53.2 %shard_map.59 = (bf16[256,2048]{1,0:T(8,128)(2,1)S(1)}, bf16[256,2048]{1,0:T(8,128)(2,1)S(1)}) custom-call(bf16[256,2048]{1,0:T(8,128)(2,1)} %a_hbm.1, bf16[2048,8192]{1,0:T(8,128)(2,1)} %w_hbm.1, bf16[256,2048]{1,0:T(8,128)(2,1)} %r_hbm.1, f32[1,2048]{1,0:T(1,128)} %bitcast.1), custom_call_target="tpu_custom_call" | custom-call | flops 8589934592 | bytes 33554432 | tf_op jit(solution)/shard_map/pallas_call | solution.py:259
  53.9 1.3 %shard_map.60 = (bf16[256,2048]{1,0:T(8,128)(2,1)}, bf16[256,2048]{1,0:T(8,128)(2,1)}) custom-call(bf16[256,2048]{1,0:T(8,128)(2,1)S(1)} %get-tuple-element.4.hid, bf16[256,2048]{1,0:T(8,128)(2,1)S(1)} %get-tuple-element.5.nrm), custom_call_target="tpu_custom_call" | custom-call | tf_op jit(solution)/shard_map/pallas_call | solution.py:283

commit v15 on v13

--- a/solution.py
+++ b/solution.py
@@ -21,8 +21,8 @@
 
 
 def kernel(d_model, a_hbm, w_hbm, r_hbm, g_hbm, hid, nrm,
-           a_v, w_v, r_v, g_v, part, recv, own, st_tx, st_rx,
-           a_sem, w0_sem, w_sem, r_sem, g_sem, far_tx, far_rx, near_tx, near_rx, sib_tx, sib_rx, stat_tx, stat_rx):
+           a_v, w_v, r_v, g_v, part, recv, own, last_sib, last_tx, last_rx, st_tx, st_rx,
+           a_sem, w0_sem, w_sem, r_sem, g_sem, far_tx, far_rx, near_tx, near_rx, last_sems, sib_tx, sib_rx, stat_tx, stat_rx):
     t = lax.axis_index("tp")
     core, chip = t % 2, t // 2
     rows, _ = a_v.shape
@@ -80,21 +80,29 @@
         sl = pl.ds(*blocks[b])
         return remote(part.at[NEAR, sl, :], recv.at[slot, sl, :], near_tx.at[b], near_rx.at[slot, b], near)
 
+    last = pl.ds(*blocks[-1])
+
+    def last_sib_copy():
+        return remote(part.at[NEAR, last, :], last_sib, last_sems.at[0], last_sems.at[1], sib)
+
+    def last_copy():
+        return remote(last_tx, last_rx, last_sems.at[2], last_sems.at[3], near)
+
     def sib_copy():
         return remote(part.at[SIB], recv.at[SIB], sib_tx, sib_rx, sib)
 
     def stat_copy(k, b, slot):
         return remote(st_tx.at[b], st_rx.at[slot, b], stat_tx.at[k, b], stat_rx.at[slot, b], (far, near, sib)[k])
 
+    barrier = pltpu.get_barrier_semaphore()
+    for p in (far, near, sib):
+        pl.semaphore_signal(barrier, inc=1, device_id={"tp": p}, device_id_type=MESH)
     a_copy(0).start()
     w0_copy(0).start()
     w0_copy(1).start()
     a_copy(1).start()
     r_copy = pltpu.make_async_copy(r_hbm, r_v, r_sem)
     g_copy = pltpu.make_async_copy(g_hbm, g_v, g_sem)
-    barrier = pltpu.get_barrier_semaphore()
-    for p in (far, near, sib):
-        pl.semaphore_signal(barrier, inc=1, device_id={"tp": p}, device_id_type=MESH)
 
     def dot(lhs, rhs):
         return jnp.dot(lhs, rhs, preferred_element_type=F32)
@@ -138,8 +146,13 @@
     def _(j):
         part[NEAR, :, columns(j)] = chunk(per + j, cross_col(per + j)).astype(BF16)
 
-    for b in range(n_blk):
+    for b in range(n_blk - 1):
         near_copy(b, core).start()
+
+    @pl.when(core == 0)
+    def _():
+        last_sib_copy().start()
+
     r_copy.start()
     g_copy.start()
 
@@ -149,6 +162,12 @@
 
     sib_copy().start()
 
+    @pl.when(core == 1)
+    def _():
+        last_sib_copy().wait_recv()
+        last_tx[...] = part[NEAR, last, :].astype(F32) + last_sib[...].astype(F32)
+        last_copy().start()
+
     @pl.loop(0, per)
     def _(j):
         own[:, columns(j)] = chunk(3 * per + j, home_col(per + j))
@@ -162,6 +181,7 @@
         for q in range(len(far_parts)):
             for slot in range(2):
                 far_copy(q, slot).wait_recv()
+        last_rx[...] = recv[0, last, :].astype(F32) + recv[1, last, :].astype(F32)
 
     lane = lax.broadcasted_iota(jnp.int32, (8, 128), 1)
     sub = lax.broadcasted_iota(jnp.int32, (8, 128), 0)
@@ -169,15 +189,21 @@
     def reduce_block(b):
         @pl.when(core == 1)
         def _():
-            for slot in range(2):
-                near_copy(b, slot).wait_recv()
+            if b == n_blk - 1:
+                last_copy().wait_recv()
+            else:
+                for slot in range(2):
+                    near_copy(b, slot).wait_recv()
 
         row, n = blocks[b]
         line = jnp.zeros((8, 128), F32)
         for first in range(0, n, SUB):
             sl = pl.ds(row + first, SUB)
-            h = own[sl, :] + recv[SIB, sl, :].astype(F32) + recv[0, sl, :].astype(F32) + recv[1, sl, :].astype(F32)
-            h = r_v[sl, :].astype(F32) + h
+            if b == n_blk - 1:
+                off_chip = last_rx[pl.ds(first, SUB), :]
+            else:
+                off_chip = recv[0, sl, :].astype(F32) + recv[1, sl, :].astype(F32)
+            h = r_v[sl, :].astype(F32) + ((own[sl, :] + recv[SIB, sl, :].astype(F32)) + off_chip)
             own[sl, :] = h
             hid[sl, :] = h.astype(BF16)
             s = jnp.sum(h * h, axis=1, keepdims=True)
@@ -209,8 +235,18 @@
 
     for q in range(len(far_parts)):
         far_copy(q, core).wait_send()
+    for b in range(n_blk - 1):
+        near_copy(b, core).wait_send()
+
+    @pl.when(core == 0)
+    def _():
+        last_sib_copy().wait_send()
+
+    @pl.when(core == 1)
+    def _():
+        last_copy().wait_send()
+
     for b in range(n_blk):
-        near_copy(b, core).wait_send()
         for k in range(3):
             stat_copy(k, b, SIB if k == SIB else core).wait_send()
     sib_copy().wait_send()
@@ -253,10 +289,13 @@
                 pltpu.VMEM((3, rows, d_loc), BF16),
                 pltpu.VMEM((3, rows, d_loc), BF16),
                 pltpu.VMEM((rows, d_loc), F32),
+                pltpu.VMEM((BLOCKS[-1], d_loc), BF16),
+                pltpu.VMEM((BLOCKS[-1], d_loc), F32),
+                pltpu.VMEM((BLOCKS[-1], d_loc), F32),
                 pltpu.VMEM((n_blk, 1, 128), F32),
                 pltpu.VMEM((3, n_blk, 1, 128), F32),
                 dma((2,)), dma((2,)), dma((4 * per,)), dma, dma,
-                dma((N_COL + 3,)), dma((2, N_COL + 3)), dma((n_blk,)), dma((2, n_blk)), dma, dma,
+                dma((N_COL + 3,)), dma((2, N_COL + 3)), dma((n_blk - 1,)), dma((2, n_blk - 1)), dma((4,)), dma, dma,
                 dma((3, n_blk)), dma((3, n_blk)),
             ],
             compiler_params=pltpu.CompilerParams(

time: 55.1 us -> 55.2 us (level)
  no operation moved by 1% of the time
where the time goes in v15:
time: 55.2 us; the launch traced here: 55 us
  Pallas kernels  54.4 us (99%)
  between operations  0.64 us (1%)
    pallas_call x1, Pallas kernels, local_step(): pl.pallas_call(functools.partial(kernel, d_loc * tp), out_shape=(pltpu.VM...  53.1 us
    pallas_call x1, Pallas kernels, local_step(): pl.pallas_call(put, out_shape=(jax.ShapeDtypeStruct((rows, d_loc), BF16),...  1.33 us

profile of v15, /device:TPU:0, one launch (start us, length us, event | category | flops | bytes accessed | tf_op | source)
XLA Modules:
  0.0 55.0 jit_solution(3600372547341600065)
XLA Ops:
  0.6 53.1 %shard_map.59 = (bf16[256,2048]{1,0:T(8,128)(2,1)S(1)}, bf16[256,2048]{1,0:T(8,128)(2,1)S(1)}) custom-call(bf16[256,2048]{1,0:T(8,128)(2,1)} %a_hbm.1, bf16[2048,8192]{1,0:T(8,128)(2,1)} %w_hbm.1, bf16[256,2048]{1,0:T(8,128)(2,1)} %r_hbm.1, f32[1,2048]{1,0:T(1,128)} %bitcast.1), custom_call_target="tpu_custom_call" | custom-call | flops 8589934592 | bytes 33554432 | tf_op jit(solution)/shard_map/pallas_call | solution.py:279
  53.7 1.3 %shard_map.60 = (bf16[256,2048]{1,0:T(8,128)(2,1)}, bf16[256,2048]{1,0:T(8,128)(2,1)}) custom-call(bf16[256,2048]{1,0:T(8,128)(2,1)S(1)} %get-tuple-element.4.hid, bf16[256,2048]{1,0:T(8,128)(2,1)S(1)} %get-tuple-element.5.nrm), custom_call_target="tpu_custom_call" | custom-call | tf_op jit(solution)/shard_map/pallas_call | solution.py:306

commit v16 on v15

--- a/solution.py
+++ b/solution.py
@@ -13,7 +13,8 @@
 
 CW = 256
 N_COL = 2
-BLOCKS = (128, 112, 16)
+BLOCKS = (128, 16, 96, 16)
+MID = 1
 SUB = 16
 DEPTH = 4
 PUT = 1
@@ -21,8 +22,8 @@
 
 
 def kernel(d_model, a_hbm, w_hbm, r_hbm, g_hbm, hid, nrm,
-           a_v, w_v, r_v, g_v, part, recv, own, last_sib, last_tx, last_rx, st_tx, st_rx,
-           a_sem, w0_sem, w_sem, r_sem, g_sem, far_tx, far_rx, near_tx, near_rx, last_sems, sib_tx, sib_rx, stat_tx, stat_rx):
+           a_v, w_v, r_v, g_v, part, recv, own, mid_sib, mid_tx, mid_rx, st_tx, st_rx,
+           a_sem, w0_sem, w_sem, r_sem, g_sem, far_tx, far_rx, near_tx, near_rx, mid_sems, sib_tx, sib_rx, stat_tx, stat_rx):
     t = lax.axis_index("tp")
     core, chip = t % 2, t // 2
     rows, _ = a_v.shape
@@ -80,13 +81,13 @@
         sl = pl.ds(*blocks[b])
         return remote(part.at[NEAR, sl, :], recv.at[slot, sl, :], near_tx.at[b], near_rx.at[slot, b], near)
 
-    last = pl.ds(*blocks[-1])
-
-    def last_sib_copy():
-        return remote(part.at[NEAR, last, :], last_sib, last_sems.at[0], last_sems.at[1], sib)
-
-    def last_copy():
-        return remote(last_tx, last_rx, last_sems.at[2], last_sems.at[3], near)
+    mid = pl.ds(*blocks[MID])
+
+    def mid_sib_copy():
+        return remote(part.at[NEAR, mid, :], mid_sib, mid_sems.at[0], mid_sems.at[1], sib)
+
+    def mid_copy():
+        return remote(mid_tx, mid_rx, mid_sems.at[2], mid_sems.at[3], near)
 
     def sib_copy():
         return remote(part.at[SIB], recv.at[SIB], sib_tx, sib_rx, sib)
@@ -146,12 +147,17 @@
     def _(j):
         part[NEAR, :, columns(j)] = chunk(per + j, cross_col(per + j)).astype(BF16)
 
-    for b in range(n_blk - 1):
-        near_copy(b, core).start()
+    plain = [b for b in range(n_blk) if b != MID]
 
     @pl.when(core == 0)
     def _():
-        last_sib_copy().start()
+        for b in plain:
+            near_copy(b, core).start()
+        mid_sib_copy().start()
+
+    @pl.when(core == 1)
+    def _():
+        near_copy(0, core).start()
 
     r_copy.start()
     g_copy.start()
@@ -164,9 +170,11 @@
 
     @pl.when(core == 1)
     def _():
-        last_sib_copy().wait_recv()
-        last_tx[...] = part[NEAR, last, :].astype(F32) + last_sib[...].astype(F32)
-        last_copy().start()
+        mid_sib_copy().wait_recv()
+        mid_tx[...] = part[NEAR, mid, :].astype(F32) + mid_sib[...].astype(F32)
+        mid_copy().start()
+        for b in plain[1:]:
+            near_copy(b, core).start()
 
     @pl.loop(0, per)
     def _(j):
@@ -181,7 +189,7 @@
         for q in range(len(far_parts)):
             for slot in range(2):
                 far_copy(q, slot).wait_recv()
-        last_rx[...] = recv[0, last, :].astype(F32) + recv[1, last, :].astype(F32)
+        mid_rx[...] = recv[0, mid, :].astype(F32) + recv[1, mid, :].astype(F32)
 
     lane = lax.broadcasted_iota(jnp.int32, (8, 128), 1)
     sub = lax.broadcasted_iota(jnp.int32, (8, 128), 0)
@@ -189,8 +197,8 @@
     def reduce_block(b):
         @pl.when(core == 1)
         def _():
-            if b == n_blk - 1:
-                last_copy().wait_recv()
+            if b == MID:
+                mid_copy().wait_recv()
             else:
                 for slot in range(2):
                     near_copy(b, slot).wait_recv()
@@ -199,8 +207,8 @@
         line = jnp.zeros((8, 128), F32)
         for first in range(0, n, SUB):
             sl = pl.ds(row + first, SUB)
-            if b == n_blk - 1:
-                off_chip = last_rx[pl.ds(first, SUB), :]
+            if b == MID:
+                off_chip = mid_rx[pl.ds(first, SUB), :]
             else:
                 off_chip = recv[0, sl, :].astype(F32) + recv[1, sl, :].astype(F32)
             h = r_v[sl, :].astype(F32) + ((own[sl, :] + recv[SIB, sl, :].astype(F32)) + off_chip)
@@ -235,16 +243,16 @@
 
     for q in range(len(far_parts)):
         far_copy(q, core).wait_send()
-    for b in range(n_blk - 1):
+    for b in plain:
         near_copy(b, core).wait_send()
 
     @pl.when(core == 0)
     def _():
-        last_sib_copy().wait_send()
+        mid_sib_copy().wait_send()
 
     @pl.when(core == 1)
     def _():
-        last_copy().wait_send()
+        mid_copy().wait_send()
 
     for b in range(n_blk):
         for k in range(3):
@@ -289,13 +297,13 @@
                 pltpu.VMEM((3, rows, d_loc), BF16),
                 pltpu.VMEM((3, rows, d_loc), BF16),
                 pltpu.VMEM((rows, d_loc), F32),
-                pltpu.VMEM((BLOCKS[-1], d_loc), BF16),
-                pltpu.VMEM((BLOCKS[-1], d_loc), F32),
-                pltpu.VMEM((BLOCKS[-1], d_loc), F32),
+                pltpu.VMEM((BLOCKS[MID], d_loc), BF16),
+                pltpu.VMEM((BLOCKS[MID], d_loc), F32),
+                pltpu.VMEM((BLOCKS[MID], d_loc), F32),
                 pltpu.VMEM((n_blk, 1, 128), F32),
                 pltpu.VMEM((3, n_blk, 1, 128), F32),
                 dma((2,)), dma((2,)), dma((4 * per,)), dma, dma,
-                dma((N_COL + 3,)), dma((2, N_COL + 3)), dma((n_blk - 1,)), dma((2, n_blk - 1)), dma((4,)), dma, dma,
+                dma((N_COL + 3,)), dma((2, N_COL + 3)), dma((n_blk,)), dma((2, n_blk)), dma((4,)), dma, dma,
                 dma((3, n_blk)), dma((3, n_blk)),
             ],
             compiler_params=pltpu.CompilerParams(

time: 55.2 us -> 55.3 us (level)
  no operation moved by 1% of the time
where the time goes in v16:
time: 55.3 us; the launch traced here: 55.2 us
  Pallas kernels  54.6 us (99%)
  between operations  0.64 us (1%)
    pallas_call x1, Pallas kernels, local_step(): pl.pallas_call(functools.partial(kernel, d_loc * tp), out_shape=(pltpu.VM...  53.2 us
    pallas_call x1, Pallas kernels, local_step(): pl.pallas_call(put, out_shape=(jax.ShapeDtypeStruct((rows, d_loc), BF16),...  1.33 us

profile of v16, /device:TPU:0, one launch (start us, length us, event | category | flops | bytes accessed | tf_op | source)
XLA Modules:
  0.0 55.2 jit_solution(15983774669212191106)
XLA Ops:
  0.6 53.2 %shard_map.59 = (bf16[256,2048]{1,0:T(8,128)(2,1)S(1)}, bf16[256,2048]{1,0:T(8,128)(2,1)S(1)}) custom-call(bf16[256,2048]{1,0:T(8,128)(2,1)} %a_hbm.1, bf16[2048,8192]{1,0:T(8,128)(2,1)} %w_hbm.1, bf16[256,2048]{1,0:T(8,128)(2,1)} %r_hbm.1, f32[1,2048]{1,0:T(1,128)} %bitcast.1), custom_call_target="tpu_custom_call" | custom-call | flops 8589934592 | bytes 33554432 | tf_op jit(solution)/shard_map/pallas_call | solution.py:287
  53.9 1.3 %shard_map.60 = (bf16[256,2048]{1,0:T(8,128)(2,1)}, bf16[256,2048]{1,0:T(8,128)(2,1)}) custom-call(bf16[256,2048]{1,0:T(8,128)(2,1)S(1)} %get-tuple-element.4.hid, bf16[256,2048]{1,0:T(8,128)(2,1)S(1)} %get-tuple-element.5.nrm), custom_call_target="tpu_custom_call" | custom-call | tf_op jit(solution)/shard_map/pallas_call | solution.py:314

commit v17 on v13

--- a/solution.py
+++ b/solution.py
@@ -12,8 +12,9 @@
 F32, BF16 = jnp.float32, jnp.bfloat16
 
 CW = 256
-N_COL = 2
+N_COL = 1
 BLOCKS = (128, 112, 16)
+NEAR_ROWS = (240, 16)
 SUB = 16
 DEPTH = 4
 PUT = 1
@@ -76,8 +77,10 @@
         sl = far_parts[q]
         return remote(part.at[(FAR, *sl)], recv.at[(slot, *sl)], far_tx.at[q], far_rx.at[slot, q], far)
 
+    near_blocks = [(sum(NEAR_ROWS[:b]), NEAR_ROWS[b]) for b in range(len(NEAR_ROWS))]
+
     def near_copy(b, slot):
-        sl = pl.ds(*blocks[b])
+        sl = pl.ds(*near_blocks[b])
         return remote(part.at[NEAR, sl, :], recv.at[slot, sl, :], near_tx.at[b], near_rx.at[slot, b], near)
 
     def sib_copy():
@@ -86,15 +89,15 @@
     def stat_copy(k, b, slot):
         return remote(st_tx.at[b], st_rx.at[slot, b], stat_tx.at[k, b], stat_rx.at[slot, b], (far, near, sib)[k])
 
+    barrier = pltpu.get_barrier_semaphore()
+    for p in (far, near, sib):
+        pl.semaphore_signal(barrier, inc=1, device_id={"tp": p}, device_id_type=MESH)
     a_copy(0).start()
     w0_copy(0).start()
     w0_copy(1).start()
     a_copy(1).start()
     r_copy = pltpu.make_async_copy(r_hbm, r_v, r_sem)
     g_copy = pltpu.make_async_copy(g_hbm, g_v, g_sem)
-    barrier = pltpu.get_barrier_semaphore()
-    for p in (far, near, sib):
-        pl.semaphore_signal(barrier, inc=1, device_id={"tp": p}, device_id_type=MESH)
 
     def dot(lhs, rhs):
         return jnp.dot(lhs, rhs, preferred_element_type=F32)
@@ -138,7 +141,7 @@
     def _(j):
         part[NEAR, :, columns(j)] = chunk(per + j, cross_col(per + j)).astype(BF16)
 
-    for b in range(n_blk):
+    for b in range(len(NEAR_ROWS)):
         near_copy(b, core).start()
     r_copy.start()
     g_copy.start()
@@ -167,12 +170,13 @@
     sub = lax.broadcasted_iota(jnp.int32, (8, 128), 0)
 
     def reduce_block(b):
-        @pl.when(core == 1)
-        def _():
-            for slot in range(2):
-                near_copy(b, slot).wait_recv()
-
         row, n = blocks[b]
+        if row in [first for first, _ in near_blocks]:
+            @pl.when(core == 1)
+            def _():
+                for slot in range(2):
+                    near_copy([first for first, _ in near_blocks].index(row), slot).wait_recv()
+
         line = jnp.zeros((8, 128), F32)
         for first in range(0, n, SUB):
             sl = pl.ds(row + first, SUB)
@@ -209,8 +213,9 @@
 
     for q in range(len(far_parts)):
         far_copy(q, core).wait_send()
+    for b in range(len(NEAR_ROWS)):
+        near_copy(b, core).wait_send()
     for b in range(n_blk):
-        near_copy(b, core).wait_send()
         for k in range(3):
             stat_copy(k, b, SIB if k == SIB else core).wait_send()
     sib_copy().wait_send()
@@ -256,7 +261,7 @@
                 pltpu.VMEM((n_blk, 1, 128), F32),
                 pltpu.VMEM((3, n_blk, 1, 128), F32),
                 dma((2,)), dma((2,)), dma((4 * per,)), dma, dma,
-                dma((N_COL + 3,)), dma((2, N_COL + 3)), dma((n_blk,)), dma((2, n_blk)), dma, dma,
+                dma((N_COL + 3,)), dma((2, N_COL + 3)), dma((len(NEAR_ROWS),)), dma((2, len(NEAR_ROWS))), dma, dma,
                 dma((3, n_blk)), dma((3, n_blk)),
             ],
             compiler_params=pltpu.CompilerParams(

time: 55.1 us -> 56.2 us (1.020)
  Pallas kernels: 54.4 us -> 55.4 us
    pallas_call x1, Pallas kernels: 53 us -> 54.1 us  [local_step(): pl.pallas_call(functools.partial(kernel, d_loc * tp), out_shape=(pltpu.VM...]
where the time goes in v17:
time: 56.2 us; the launch traced here: 56.1 us
  Pallas kernels  55.4 us (99%)
  between operations  0.64 us (1%)
    pallas_call x1, Pallas kernels, local_step(): pl.pallas_call(functools.partial(kernel, d_loc * tp), out_shape=(pltpu.VM...  54.1 us
    pallas_call x1, Pallas kernels, local_step(): pl.pallas_call(put, out_shape=(jax.ShapeDtypeStruct((rows, d_loc), BF16),...  1.33 us

profile of v17, /device:TPU:0, one launch (start us, length us, event | category | flops | bytes accessed | tf_op | source)
XLA Modules:
  0.0 56.1 jit_solution(5866226455642247050)
XLA Ops:
  0.6 54.1 %shard_map.59 = (bf16[256,2048]{1,0:T(8,128)(2,1)S(1)}, bf16[256,2048]{1,0:T(8,128)(2,1)S(1)}) custom-call(bf16[256,2048]{1,0:T(8,128)(2,1)} %a_hbm.1, bf16[2048,8192]{1,0:T(8,128)(2,1)} %w_hbm.1, bf16[256,2048]{1,0:T(8,128)(2,1)} %r_hbm.1, f32[1,2048]{1,0:T(1,128)} %bitcast.1), custom_call_target="tpu_custom_call" | custom-call | flops 8589934592 | bytes 33554432 | tf_op jit(solution)/shard_map/pallas_call | solution.py:248
  54.7 1.3 %shard_map.60 = (bf16[256,2048]{1,0:T(8,128)(2,1)}, bf16[256,2048]{1,0:T(8,128)(2,1)}) custom-call(bf16[256,2048]{1,0:T(8,128)(2,1)S(1)} %get-tuple-element.4.hid, bf16[256,2048]{1,0:T(8,128)(2,1)S(1)} %get-tuple-element.5.nrm), custom_call_target="tpu_custom_call" | custom-call | tf_op jit(solution)/shard_map/pallas_call | solution.py:272

commit v18 on v17

--- a/solution.py
+++ b/solution.py
@@ -12,7 +12,7 @@
 F32, BF16 = jnp.float32, jnp.bfloat16
 
 CW = 256
-N_COL = 1
+N_COL = 2
 BLOCKS = (128, 112, 16)
 NEAR_ROWS = (240, 16)
 SUB = 16

time: 56.2 us -> 55.1 us (0.980)
  Pallas kernels: 55.4 us -> 54.3 us
    pallas_call x1, Pallas kernels: 54.1 us -> 53 us  [local_step(): pl.pallas_call(functools.partial(kernel, d_loc * tp), out_shape=(pltpu.VM...]
where the time goes in v18:
time: 55.1 us; the launch traced here: 55 us
  Pallas kernels  54.3 us (99%)
  between operations  0.64 us (1%)
    pallas_call x1, Pallas kernels, local_step(): pl.pallas_call(functools.partial(kernel, d_loc * tp), out_shape=(pltpu.VM...  53 us
    pallas_call x1, Pallas kernels, local_step(): pl.pallas_call(put, out_shape=(jax.ShapeDtypeStruct((rows, d_loc), BF16),...  1.33 us

profile of v18, /device:TPU:0, one launch (start us, length us, event | category | flops | bytes accessed | tf_op | source)
XLA Modules:
  0.0 55.0 jit_solution(10608296563792878464)
XLA Ops:
  0.6 53.0 %shard_map.59 = (bf16[256,2048]{1,0:T(8,128)(2,1)S(1)}, bf16[256,2048]{1,0:T(8,128)(2,1)S(1)}) custom-call(bf16[256,2048]{1,0:T(8,128)(2,1)} %a_hbm.1, bf16[2048,8192]{1,0:T(8,128)(2,1)} %w_hbm.1, bf16[256,2048]{1,0:T(8,128)(2,1)} %r_hbm.1, f32[1,2048]{1,0:T(1,128)} %bitcast.1), custom_call_target="tpu_custom_call" | custom-call | flops 8589934592 | bytes 33554432 | tf_op jit(solution)/shard_map/pallas_call | solution.py:248
  53.6 1.3 %shard_map.60 = (bf16[256,2048]{1,0:T(8,128)(2,1)}, bf16[256,2048]{1,0:T(8,128)(2,1)}) custom-call(bf16[256,2048]{1,0:T(8,128)(2,1)S(1)} %get-tuple-element.4.hid, bf16[256,2048]{1,0:T(8,128)(2,1)S(1)} %get-tuple-element.5.nrm), custom_call_target="tpu_custom_call" | custom-call | tf_op jit(solution)/shard_map/pallas_call | solution.py:272

commit v19 on v16

--- a/solution.py
+++ b/solution.py
@@ -13,8 +13,9 @@
 
 CW = 256
 N_COL = 2
-BLOCKS = (128, 16, 96, 16)
-MID = 1
+BLOCKS = (128, 112, 16)
+NEAR_ROWS = (96, 144, 16)
+MID = 128
 SUB = 16
 DEPTH = 4
 PUT = 1
@@ -77,14 +78,16 @@
         sl = far_parts[q]
         return remote(part.at[(FAR, *sl)], recv.at[(slot, *sl)], far_tx.at[q], far_rx.at[slot, q], far)
 
+    near_blocks = [(sum(NEAR_ROWS[:b]), NEAR_ROWS[b]) for b in range(len(NEAR_ROWS))]
+
     def near_copy(b, slot):
-        sl = pl.ds(*blocks[b])
-        return remote(part.at[NEAR, sl, :], recv.at[slot, sl, :], near_tx.at[b], near_rx.at[slot, b], near)
-
-    mid = pl.ds(*blocks[MID])
+        sl = (pl.ds(*near_blocks[b]), pl.ds(0, d_loc if b else d_loc - MID))
+        return remote(part.at[(NEAR, *sl)], recv.at[(slot, *sl)], near_tx.at[b], near_rx.at[slot, b], near)
+
+    mid = (pl.ds(0, NEAR_ROWS[0]), pl.ds(d_loc - MID, MID))
 
     def mid_sib_copy():
-        return remote(part.at[NEAR, mid, :], mid_sib, mid_sems.at[0], mid_sems.at[1], sib)
+        return remote(part.at[(NEAR, *mid)], mid_sib, mid_sems.at[0], mid_sems.at[1], sib)
 
     def mid_copy():
         return remote(mid_tx, mid_rx, mid_sems.at[2], mid_sems.at[3], near)
@@ -147,17 +150,13 @@
     def _(j):
         part[NEAR, :, columns(j)] = chunk(per + j, cross_col(per + j)).astype(BF16)
 
-    plain = [b for b in range(n_blk) if b != MID]
+    near_copy(0, core).start()
 
     @pl.when(core == 0)
     def _():
-        for b in plain:
+        for b in range(1, len(NEAR_ROWS)):
             near_copy(b, core).start()
         mid_sib_copy().start()
-
-    @pl.when(core == 1)
-    def _():
-        near_copy(0, core).start()
 
     r_copy.start()
     g_copy.start()
@@ -171,9 +170,9 @@
     @pl.when(core == 1)
     def _():
         mid_sib_copy().wait_recv()
-        mid_tx[...] = part[NEAR, mid, :].astype(F32) + mid_sib[...].astype(F32)
+        mid_tx[...] = part[(NEAR, *mid)].astype(F32) + mid_sib[...].astype(F32)
         mid_copy().start()
-        for b in plain[1:]:
+        for b in range(1, len(NEAR_ROWS)):
             near_copy(b, core).start()
 
     @pl.loop(0, per)
@@ -189,29 +188,32 @@
         for q in range(len(far_parts)):
             for slot in range(2):
                 far_copy(q, slot).wait_recv()
-        mid_rx[...] = recv[0, mid, :].astype(F32) + recv[1, mid, :].astype(F32)
 
     lane = lax.broadcasted_iota(jnp.int32, (8, 128), 1)
     sub = lax.broadcasted_iota(jnp.int32, (8, 128), 0)
 
+    use = [min(b for b in range(n_blk) if blocks[b][0] < first + m and first < sum(blocks[b])) for first, m in near_blocks]
+
     def reduce_block(b):
+        row, n = blocks[b]
+
         @pl.when(core == 1)
         def _():
-            if b == MID:
+            if b == 0:
                 mid_copy().wait_recv()
-            else:
+                own[mid] = own[mid] + mid_rx[...]
                 for slot in range(2):
-                    near_copy(b, slot).wait_recv()
-
-        row, n = blocks[b]
+                    recv[(slot, *mid)] = jnp.zeros_like(mid_sib)
+            for q in range(len(near_blocks)):
+                if use[q] == b:
+                    for slot in range(2):
+                        near_copy(q, slot).wait_recv()
+
         line = jnp.zeros((8, 128), F32)
         for first in range(0, n, SUB):
             sl = pl.ds(row + first, SUB)
-            if b == MID:
-                off_chip = mid_rx[pl.ds(first, SUB), :]
-            else:
-                off_chip = recv[0, sl, :].astype(F32) + recv[1, sl, :].astype(F32)
-            h = r_v[sl, :].astype(F32) + ((own[sl, :] + recv[SIB, sl, :].astype(F32)) + off_chip)
+            h = own[sl, :] + recv[SIB, sl, :].astype(F32) + recv[0, sl, :].astype(F32) + recv[1, sl, :].astype(F32)
+            h = r_v[sl, :].astype(F32) + h
             own[sl, :] = h
             hid[sl, :] = h.astype(BF16)
             s = jnp.sum(h * h, axis=1, keepdims=True)
@@ -243,7 +245,7 @@
 
     for q in range(len(far_parts)):
         far_copy(q, core).wait_send()
-    for b in plain:
+    for b in range(len(NEAR_ROWS)):
         near_copy(b, core).wait_send()
 
     @pl.when(core == 0)
@@ -297,13 +299,13 @@
                 pltpu.VMEM((3, rows, d_loc), BF16),
                 pltpu.VMEM((3, rows, d_loc), BF16),
                 pltpu.VMEM((rows, d_loc), F32),
-                pltpu.VMEM((BLOCKS[MID], d_loc), BF16),
-                pltpu.VMEM((BLOCKS[MID], d_loc), F32),
-                pltpu.VMEM((BLOCKS[MID], d_loc), F32),
+                pltpu.VMEM((NEAR_ROWS[0], MID), BF16),
+                pltpu.VMEM((NEAR_ROWS[0], MID), F32),
+                pltpu.VMEM((NEAR_ROWS[0], MID), F32),
                 pltpu.VMEM((n_blk, 1, 128), F32),
                 pltpu.VMEM((3, n_blk, 1, 128), F32),
                 dma((2,)), dma((2,)), dma((4 * per,)), dma, dma,
-                dma((N_COL + 3,)), dma((2, N_COL + 3)), dma((n_blk,)), dma((2, n_blk)), dma((4,)), dma, dma,
+                dma((N_COL + 3,)), dma((2, N_COL + 3)), dma((len(NEAR_ROWS),)), dma((2, len(NEAR_ROWS))), dma((4,)), dma, dma,
                 dma((3, n_blk)), dma((3, n_blk)),
             ],
             compiler_params=pltpu.CompilerParams(

time: 55.3 us -> 55.1 us (level)
  no operation moved by 1% of the time
where the time goes in v19:
time: 55.1 us; the launch traced here: 55 us
  Pallas kernels  54.4 us (99%)
  between operations  0.64 us (1%)
    pallas_call x1, Pallas kernels, local_step(): pl.pallas_call(functools.partial(kernel, d_loc * tp), out_shape=(pltpu.VM...  53 us
    pallas_call x1, Pallas kernels, local_step(): pl.pallas_call(put, out_shape=(jax.ShapeDtypeStruct((rows, d_loc), BF16),...  1.33 us

profile of v19, /device:TPU:0, one launch (start us, length us, event | category | flops | bytes accessed | tf_op | source)
XLA Modules:
  0.0 55.0 jit_solution(1339116333479873170)
XLA Ops:
  0.6 53.0 %shard_map.59 = (bf16[256,2048]{1,0:T(8,128)(2,1)S(1)}, bf16[256,2048]{1,0:T(8,128)(2,1)S(1)}) custom-call(bf16[256,2048]{1,0:T(8,128)(2,1)} %a_hbm.1, bf16[2048,8192]{1,0:T(8,128)(2,1)} %w_hbm.1, bf16[256,2048]{1,0:T(8,128)(2,1)} %r_hbm.1, f32[1,2048]{1,0:T(1,128)} %bitcast.1), custom_call_target="tpu_custom_call" | custom-call | flops 8589934592 | bytes 33554432 | tf_op jit(solution)/shard_map/pallas_call | solution.py:289
  53.7 1.3 %shard_map.60 = (bf16[256,2048]{1,0:T(8,128)(2,1)}, bf16[256,2048]{1,0:T(8,128)(2,1)}) custom-call(bf16[256,2048]{1,0:T(8,128)(2,1)S(1)} %get-tuple-element.4.hid, bf16[256,2048]{1,0:T(8,128)(2,1)S(1)} %get-tuple-element.5.nrm), custom_call_target="tpu_custom_call" | custom-call | tf_op jit(solution)/shard_map/pallas_call | solution.py:316

commit v20 on v18

--- a/solution.py
+++ b/solution.py
@@ -23,7 +23,7 @@
 
 def kernel(d_model, a_hbm, w_hbm, r_hbm, g_hbm, hid, nrm,
            a_v, w_v, r_v, g_v, part, recv, own, st_tx, st_rx,
-           a_sem, w0_sem, w_sem, r_sem, g_sem, far_tx, far_rx, near_tx, near_rx, sib_tx, sib_rx, stat_tx, stat_rx):
+           a_sem, w_sem, r_sem, g_sem, far_tx, far_rx, near_tx, near_rx, sib_tx, sib_rx, stat_tx, stat_rx):
     t = lax.axis_index("tp")
     core, chip = t % 2, t // 2
     rows, _ = a_v.shape
@@ -31,7 +31,6 @@
     per = d_loc // CW
     n_blk = len(BLOCKS)
     blocks = [(sum(BLOCKS[:b]), BLOCKS[b]) for b in range(n_blk)]
-    half, lanes = rows // 2, 128
     far, near, sib = 2 - 2 * chip, 3 - 2 * chip, t + 1 - 2 * core
 
     def cross_col(i):
@@ -56,21 +55,14 @@
         def _():
             w_copy(i, home_col(i - 2 * per)).start()
 
-    def a_copy(q):
-        sl = pl.ds(q * half, half)
-        return pltpu.make_async_copy(a_hbm.at[sl, :], a_v.at[sl, :], a_sem.at[q])
-
-    def w0_copy(q):
-        src = w_hbm.at[:, pl.ds(pl.multiple_of(far * d_loc + q * lanes, lanes), lanes)]
-        return pltpu.make_async_copy(src, w_v.at[0, :, pl.ds(q * lanes, lanes)], w0_sem.at[q])
+    a_copy = pltpu.make_async_copy(a_hbm, a_v, a_sem)
 
     def remote(src, dst, tx, rx, peer):
         return pltpu.make_async_remote_copy(src_ref=src, dst_ref=dst, send_sem=tx, recv_sem=rx,
                                             device_id={"tp": peer}, device_id_type=MESH)
 
     every = pl.ds(0, rows)
-    far_parts = [(pl.ds(0, half), pl.ds(0, lanes)), (pl.ds(0, half), pl.ds(lanes, lanes)), (pl.ds(half, half), pl.ds(0, CW))]
-    far_parts += [(every, pl.ds(j * CW, CW)) for j in range(1, N_COL)]
+    far_parts = [(every, pl.ds(j * CW, CW)) for j in range(N_COL)]
     far_parts += [(every, pl.ds(N_COL * CW, d_loc - N_COL * CW))]
 
     def far_copy(q, slot):
@@ -92,32 +84,15 @@
     barrier = pltpu.get_barrier_semaphore()
     for p in (far, near, sib):
         pl.semaphore_signal(barrier, inc=1, device_id={"tp": p}, device_id_type=MESH)
-    a_copy(0).start()
-    w0_copy(0).start()
-    w0_copy(1).start()
-    a_copy(1).start()
+    w_start(0)
+    a_copy.start()
+    for i in range(1, DEPTH):
+        w_start(i)
     r_copy = pltpu.make_async_copy(r_hbm, r_v, r_sem)
     g_copy = pltpu.make_async_copy(g_hbm, g_v, g_sem)
 
     def dot(lhs, rhs):
         return jnp.dot(lhs, rhs, preferred_element_type=F32)
-
-    for q in range(3):
-        if q == 0:
-            a_copy(0).wait()
-            w0_copy(0).wait()
-            for i in range(1, DEPTH):
-                w_start(i)
-        elif q == 1:
-            w0_copy(1).wait()
-        else:
-            a_copy(1).wait()
-            w_start(DEPTH)
-        r_sl, c_sl = far_parts[q]
-        part[FAR, r_sl, c_sl] = dot(a_v[r_sl, :], w_v[0, :, c_sl]).astype(BF16)
-        if q == 0:
-            pl.semaphore_wait(barrier, 3)
-        far_copy(q, core).start()
 
     def chunk(i, col):
         w_copy(i, col).wait()
@@ -127,9 +102,13 @@
     def columns(j):
         return pl.ds(pl.multiple_of(j * CW, CW), CW)
 
-    for j in range(1, N_COL):
+    for j in range(N_COL):
+        if j == 0:
+            a_copy.wait()
         part[FAR, :, columns(j)] = chunk(j, cross_col(j)).astype(BF16)
-        far_copy(2 + j, core).start()
+        if j == 0:
+            pl.semaphore_wait(barrier, 3)
+        far_copy(j, core).start()
 
     @pl.loop(N_COL, per)
     def _(j):
@@ -260,8 +239,8 @@
                 pltpu.VMEM((rows, d_loc), F32),
                 pltpu.VMEM((n_blk, 1, 128), F32),
                 pltpu.VMEM((3, n_blk, 1, 128), F32),
-                dma((2,)), dma((2,)), dma((4 * per,)), dma, dma,
-                dma((N_COL + 3,)), dma((2, N_COL + 3)), dma((len(NEAR_ROWS),)), dma((2, len(NEAR_ROWS))), dma, dma,
+                dma, dma((4 * per,)), dma, dma,
+                dma((N_COL + 1,)), dma((2, N_COL + 1)), dma((len(NEAR_ROWS),)), dma((2, len(NEAR_ROWS))), dma, dma,
                 dma((3, n_blk)), dma((3, n_blk)),
             ],
             compiler_params=pltpu.CompilerParams(

time: 55.1 us -> 55.5 us (level)
  no operation moved by 1% of the time
where the time goes in v20:
time: 55.5 us; the launch traced here: 55.4 us
  Pallas kernels  54.8 us (99%)
  between operations  0.64 us (1%)
    pallas_call x1, Pallas kernels, local_step(): pl.pallas_call(functools.partial(kernel, d_loc * tp), out_shape=(pltpu.VM...  53.5 us
    pallas_call x1, Pallas kernels, local_step(): pl.pallas_call(put, out_shape=(jax.ShapeDtypeStruct((rows, d_loc), BF16),...  1.33 us

profile of v20, /device:TPU:0, one launch (start us, length us, event | category | flops | bytes accessed | tf_op | source)
XLA Modules:
  0.0 55.4 jit_solution(4152603648469014436)
XLA Ops:
  0.6 53.5 %shard_map.59 = (bf16[256,2048]{1,0:T(8,128)(2,1)S(1)}, bf16[256,2048]{1,0:T(8,128)(2,1)S(1)}) custom-call(bf16[256,2048]{1,0:T(8,128)(2,1)} %a_hbm.1, bf16[2048,8192]{1,0:T(8,128)(2,1)} %w_hbm.1, bf16[256,2048]{1,0:T(8,128)(2,1)} %r_hbm.1, f32[1,2048]{1,0:T(1,128)} %bitcast.1), custom_call_target="tpu_custom_call" | custom-call | flops 8589934592 | bytes 33554432 | tf_op jit(solution)/shard_map/pallas_call | solution.py:227
  54.1 1.3 %shard_map.60 = (bf16[256,2048]{1,0:T(8,128)(2,1)}, bf16[256,2048]{1,0:T(8,128)(2,1)}) custom-call(bf16[256,2048]{1,0:T(8,128)(2,1)S(1)} %get-tuple-element.4.hid, bf16[256,2048]{1,0:T(8,128)(2,1)S(1)} %get-tuple-element.5.nrm), custom_call_target="tpu_custom_call" | custom-call | tf_op jit(solution)/shard_map/pallas_call | solution.py:251

commit v21 on v18

--- a/solution.py
+++ b/solution.py
@@ -12,18 +12,20 @@
 F32, BF16 = jnp.float32, jnp.bfloat16
 
 CW = 256
+FIRST = 64
 N_COL = 2
 BLOCKS = (128, 112, 16)
 NEAR_ROWS = (240, 16)
 SUB = 16
 DEPTH = 4
 PUT = 1
-FAR, NEAR, SIB = 0, 1, 2
+NEAR, SIB = 0, 1
+FROM_SIB = 2
 
 
 def kernel(d_model, a_hbm, w_hbm, r_hbm, g_hbm, hid, nrm,
-           a_v, w_v, r_v, g_v, part, recv, own, st_tx, st_rx,
-           a_sem, w0_sem, w_sem, r_sem, g_sem, far_tx, far_rx, near_tx, near_rx, sib_tx, sib_rx, stat_tx, stat_rx):
+           a_v, w_v, r_v, g_v, far_part, far_recv, part, recv, own, st_tx, st_rx,
+           a_sem, w_sem, r_sem, g_sem, far_tx, far_rx, near_tx, near_rx, sib_tx, sib_rx, stat_tx, stat_rx):
     t = lax.axis_index("tp")
     core, chip = t % 2, t // 2
     rows, _ = a_v.shape
@@ -31,7 +33,6 @@
     per = d_loc // CW
     n_blk = len(BLOCKS)
     blocks = [(sum(BLOCKS[:b]), BLOCKS[b]) for b in range(n_blk)]
-    half, lanes = rows // 2, 128
     far, near, sib = 2 - 2 * chip, 3 - 2 * chip, t + 1 - 2 * core
 
     def cross_col(i):
@@ -57,25 +58,21 @@
             w_copy(i, home_col(i - 2 * per)).start()
 
     def a_copy(q):
-        sl = pl.ds(q * half, half)
+        sl = pl.ds(*((0, FIRST), (FIRST, rows - FIRST))[q])
         return pltpu.make_async_copy(a_hbm.at[sl, :], a_v.at[sl, :], a_sem.at[q])
-
-    def w0_copy(q):
-        src = w_hbm.at[:, pl.ds(pl.multiple_of(far * d_loc + q * lanes, lanes), lanes)]
-        return pltpu.make_async_copy(src, w_v.at[0, :, pl.ds(q * lanes, lanes)], w0_sem.at[q])
 
     def remote(src, dst, tx, rx, peer):
         return pltpu.make_async_remote_copy(src_ref=src, dst_ref=dst, send_sem=tx, recv_sem=rx,
                                             device_id={"tp": peer}, device_id_type=MESH)
 
     every = pl.ds(0, rows)
-    far_parts = [(pl.ds(0, half), pl.ds(0, lanes)), (pl.ds(0, half), pl.ds(lanes, lanes)), (pl.ds(half, half), pl.ds(0, CW))]
-    far_parts += [(every, pl.ds(j * CW, CW)) for j in range(1, N_COL)]
-    far_parts += [(every, pl.ds(N_COL * CW, d_loc - N_COL * CW))]
+    far_parts = [(pl.ds(0, 1), pl.ds(0, FIRST)), (pl.ds(0, 1), pl.ds(FIRST, rows - FIRST))]
+    far_parts += [(pl.ds(j, 1), every) for j in range(1, N_COL)]
+    far_parts += [(pl.ds(N_COL, per - N_COL), every)]
 
     def far_copy(q, slot):
         sl = far_parts[q]
-        return remote(part.at[(FAR, *sl)], recv.at[(slot, *sl)], far_tx.at[q], far_rx.at[slot, q], far)
+        return remote(far_part.at[sl], far_recv.at[(slot, *sl)], far_tx.at[q], far_rx.at[slot, q], far)
 
     near_blocks = [(sum(NEAR_ROWS[:b]), NEAR_ROWS[b]) for b in range(len(NEAR_ROWS))]
 
@@ -84,7 +81,7 @@
         return remote(part.at[NEAR, sl, :], recv.at[slot, sl, :], near_tx.at[b], near_rx.at[slot, b], near)
 
     def sib_copy():
-        return remote(part.at[SIB], recv.at[SIB], sib_tx, sib_rx, sib)
+        return remote(part.at[SIB], recv.at[FROM_SIB], sib_tx, sib_rx, sib)
 
     def stat_copy(k, b, slot):
         return remote(st_tx.at[b], st_rx.at[slot, b], stat_tx.at[k, b], stat_rx.at[slot, b], (far, near, sib)[k])
@@ -93,8 +90,7 @@
     for p in (far, near, sib):
         pl.semaphore_signal(barrier, inc=1, device_id={"tp": p}, device_id_type=MESH)
     a_copy(0).start()
-    w0_copy(0).start()
-    w0_copy(1).start()
+    w_start(0)
     a_copy(1).start()
     r_copy = pltpu.make_async_copy(r_hbm, r_v, r_sem)
     g_copy = pltpu.make_async_copy(g_hbm, g_v, g_sem)
@@ -102,19 +98,16 @@
     def dot(lhs, rhs):
         return jnp.dot(lhs, rhs, preferred_element_type=F32)
 
-    for q in range(3):
+    for q in range(2):
+        a_copy(q).wait()
         if q == 0:
-            a_copy(0).wait()
-            w0_copy(0).wait()
+            w_copy(0, cross_col(0)).wait()
             for i in range(1, DEPTH):
                 w_start(i)
-        elif q == 1:
-            w0_copy(1).wait()
         else:
-            a_copy(1).wait()
             w_start(DEPTH)
-        r_sl, c_sl = far_parts[q]
-        part[FAR, r_sl, c_sl] = dot(a_v[r_sl, :], w_v[0, :, c_sl]).astype(BF16)
+        sl = far_parts[q][1]
+        far_part[0, sl, :] = dot(a_v[sl, :], w_v[0]).astype(BF16)
         if q == 0:
             pl.semaphore_wait(barrier, 3)
         far_copy(q, core).start()
@@ -128,12 +121,12 @@
         return pl.ds(pl.multiple_of(j * CW, CW), CW)
 
     for j in range(1, N_COL):
-        part[FAR, :, columns(j)] = chunk(j, cross_col(j)).astype(BF16)
-        far_copy(2 + j, core).start()
+        far_part[j] = chunk(j, cross_col(j)).astype(BF16)
+        far_copy(1 + j, core).start()
 
     @pl.loop(N_COL, per)
     def _(j):
-        part[FAR, :, columns(j)] = chunk(j, cross_col(j)).astype(BF16)
+        far_part[j] = chunk(j, cross_col(j)).astype(BF16)
 
     far_copy(len(far_parts) - 1, core).start()
 
@@ -165,6 +158,13 @@
         for q in range(len(far_parts)):
             for slot in range(2):
                 far_copy(q, slot).wait_recv()
+
+        @pl.loop(0, per)
+        def _(j):
+            own[:, columns(j)] += far_recv[0, j].astype(F32) + far_recv[1, j].astype(F32)
+
+        for slot in range(2):
+            recv[slot] = jnp.zeros((rows, d_loc), BF16)
 
     lane = lax.broadcasted_iota(jnp.int32, (8, 128), 1)
     sub = lax.broadcasted_iota(jnp.int32, (8, 128), 0)
@@ -180,7 +180,7 @@
         line = jnp.zeros((8, 128), F32)
         for first in range(0, n, SUB):
             sl = pl.ds(row + first, SUB)
-            h = own[sl, :] + recv[SIB, sl, :].astype(F32) + recv[0, sl, :].astype(F32) + recv[1, sl, :].astype(F32)
+            h = own[sl, :] + recv[FROM_SIB, sl, :].astype(F32) + recv[0, sl, :].astype(F32) + recv[1, sl, :].astype(F32)
             h = r_v[sl, :].astype(F32) + h
             own[sl, :] = h
             hid[sl, :] = h.astype(BF16)
@@ -189,13 +189,13 @@
                 line = line + jnp.where(lane == sub + (first + q), s[q:q + 8, :], 0.0)
         st_tx[b] = jnp.sum(line, axis=0, keepdims=True)
         for k in range(3):
-            stat_copy(k, b, SIB if k == SIB else core).start()
+            stat_copy(k, b, k if k == 2 else core).start()
 
     def norm_block(b):
         for slot in range(3):
             stat_copy(slot, b, slot).wait_recv()
         row, n = blocks[b]
-        tot = (st_tx[b] + st_rx[SIB, b]) + (st_rx[0, b] + st_rx[1, b])
+        tot = (st_tx[b] + st_rx[2, b]) + (st_rx[0, b] + st_rx[1, b])
         scale = jnp.broadcast_to(lax.rsqrt(tot / d_model + EPS), (8, 128))
         for first in range(0, n, SUB):
             for q in range(first, first + SUB, 8):
@@ -217,7 +217,7 @@
         near_copy(b, core).wait_send()
     for b in range(n_blk):
         for k in range(3):
-            stat_copy(k, b, SIB if k == SIB else core).wait_send()
+            stat_copy(k, b, k if k == 2 else core).wait_send()
     sib_copy().wait_send()
 
 
@@ -255,13 +255,15 @@
                 pltpu.VMEM((4 * per, depth, CW), BF16),
                 pltpu.VMEM((rows, d_loc), BF16),
                 pltpu.VMEM((1, d_loc), F32),
-                pltpu.VMEM((3, rows, d_loc), BF16),
+                pltpu.VMEM((per, rows, CW), BF16),
+                pltpu.VMEM((2, per, rows, CW), BF16),
+                pltpu.VMEM((2, rows, d_loc), BF16),
                 pltpu.VMEM((3, rows, d_loc), BF16),
                 pltpu.VMEM((rows, d_loc), F32),
                 pltpu.VMEM((n_blk, 1, 128), F32),
                 pltpu.VMEM((3, n_blk, 1, 128), F32),
-                dma((2,)), dma((2,)), dma((4 * per,)), dma, dma,
-                dma((N_COL + 3,)), dma((2, N_COL + 3)), dma((len(NEAR_ROWS),)), dma((2, len(NEAR_ROWS))), dma, dma,
+                dma((2,)), dma((4 * per,)), dma, dma,
+                dma((N_COL + 2,)), dma((2, N_COL + 2)), dma((len(NEAR_ROWS),)), dma((2, len(NEAR_ROWS))), dma, dma,
                 dma((3, n_blk)), dma((3, n_blk)),
             ],
             compiler_params=pltpu.CompilerParams(

time: 55.1 us -> 55.2 us (level)
  no operation moved by 1% of the time
where the time goes in v21:
time: 55.2 us; the launch traced here: 55.1 us
  Pallas kernels  54.5 us (99%)
  between operations  0.64 us (1%)
    pallas_call x1, Pallas kernels, local_step(): pl.pallas_call(functools.partial(kernel, d_loc * tp), out_shape=(pltpu.VM...  53.1 us
    pallas_call x1, Pallas kernels, local_step(): pl.pallas_call(put, out_shape=(jax.ShapeDtypeStruct((rows, d_loc), BF16),...  1.33 us

profile of v21, /device:TPU:0, one launch (start us, length us, event | category | flops | bytes accessed | tf_op | source)
XLA Modules:
  0.0 55.1 jit_solution(1739169459182149621)
XLA Ops:
  0.6 53.1 %shard_map.59 = (bf16[256,2048]{1,0:T(8,128)(2,1)S(1)}, bf16[256,2048]{1,0:T(8,128)(2,1)S(1)}) custom-call(bf16[256,2048]{1,0:T(8,128)(2,1)} %a_hbm.1, bf16[2048,8192]{1,0:T(8,128)(2,1)} %w_hbm.1, bf16[256,2048]{1,0:T(8,128)(2,1)} %r_hbm.1, f32[1,2048]{1,0:T(1,128)} %bitcast.1), custom_call_target="tpu_custom_call" | custom-call | flops 8589934592 | bytes 33554432 | tf_op jit(solution)/shard_map/pallas_call | solution.py:248
  53.8 1.3 %shard_map.60 = (bf16[256,2048]{1,0:T(8,128)(2,1)}, bf16[256,2048]{1,0:T(8,128)(2,1)}) custom-call(bf16[256,2048]{1,0:T(8,128)(2,1)S(1)} %get-tuple-element.4.hid, bf16[256,2048]{1,0:T(8,128)(2,1)S(1)} %get-tuple-element.5.nrm), custom_call_target="tpu_custom_call" | custom-call | tf_op jit(solution)/shard_map/pallas_call | solution.py:274

commit v22 on v18

--- a/solution.py
+++ b/solution.py
@@ -15,6 +15,7 @@
 N_COL = 2
 BLOCKS = (128, 112, 16)
 NEAR_ROWS = (240, 16)
+NEAR_CUTS = (1, 4)
 SUB = 16
 DEPTH = 4
 PUT = 1
@@ -77,11 +78,14 @@
         sl = far_parts[q]
         return remote(part.at[(FAR, *sl)], recv.at[(slot, *sl)], far_tx.at[q], far_rx.at[slot, q], far)
 
-    near_blocks = [(sum(NEAR_ROWS[:b]), NEAR_ROWS[b]) for b in range(len(NEAR_ROWS))]
-
-    def near_copy(b, slot):
-        sl = pl.ds(*near_blocks[b])
-        return remote(part.at[NEAR, sl, :], recv.at[slot, sl, :], near_tx.at[b], near_rx.at[slot, b], near)
+    near_parts = []
+    for b, cuts in enumerate(NEAR_CUTS):
+        n = d_loc // cuts
+        near_parts += [(pl.ds(sum(NEAR_ROWS[:b]), NEAR_ROWS[b]), pl.ds(q * n, n)) for q in range(cuts)]
+
+    def near_copy(q, slot):
+        sl = near_parts[q]
+        return remote(part.at[(NEAR, *sl)], recv.at[(slot, *sl)], near_tx.at[q], near_rx.at[slot, q], near)
 
     def sib_copy():
         return remote(part.at[SIB], recv.at[SIB], sib_tx, sib_rx, sib)
@@ -141,8 +145,8 @@
     def _(j):
         part[NEAR, :, columns(j)] = chunk(per + j, cross_col(per + j)).astype(BF16)
 
-    for b in range(len(NEAR_ROWS)):
-        near_copy(b, core).start()
+    for q in range(len(near_parts)):
+        near_copy(q, core).start()
     r_copy.start()
     g_copy.start()
 
@@ -171,11 +175,13 @@
 
     def reduce_block(b):
         row, n = blocks[b]
-        if row in [first for first, _ in near_blocks]:
+        awaited = [q for q, (r_sl, _) in enumerate(near_parts) if r_sl.start == row]
+        if awaited:
             @pl.when(core == 1)
             def _():
-                for slot in range(2):
-                    near_copy([first for first, _ in near_blocks].index(row), slot).wait_recv()
+                for q in awaited:
+                    for slot in range(2):
+                        near_copy(q, slot).wait_recv()
 
         line = jnp.zeros((8, 128), F32)
         for first in range(0, n, SUB):
@@ -213,8 +219,8 @@
 
     for q in range(len(far_parts)):
         far_copy(q, core).wait_send()
-    for b in range(len(NEAR_ROWS)):
-        near_copy(b, core).wait_send()
+    for q in range(len(near_parts)):
+        near_copy(q, core).wait_send()
     for b in range(n_blk):
         for k in range(3):
             stat_copy(k, b, SIB if k == SIB else core).wait_send()
@@ -261,7 +267,7 @@
                 pltpu.VMEM((n_blk, 1, 128), F32),
                 pltpu.VMEM((3, n_blk, 1, 128), F32),
                 dma((2,)), dma((2,)), dma((4 * per,)), dma, dma,
-                dma((N_COL + 3,)), dma((2, N_COL + 3)), dma((len(NEAR_ROWS),)), dma((2, len(NEAR_ROWS))), dma, dma,
+                dma((N_COL + 3,)), dma((2, N_COL + 3)), dma((sum(NEAR_CUTS),)), dma((2, sum(NEAR_CUTS))), dma, dma,
                 dma((3, n_blk)), dma((3, n_blk)),
             ],
             compiler_params=pltpu.CompilerParams(

time: 55.1 us -> 55.2 us (level)
  no operation moved by 1% of the time
where the time goes in v22:
time: 55.2 us; the launch traced here: 55.1 us
  Pallas kernels  54.4 us (99%)
  between operations  0.64 us (1%)
    pallas_call x1, Pallas kernels, local_step(): pl.pallas_call(functools.partial(kernel, d_loc * tp), out_shape=(pltpu.VM...  53.1 us
    pallas_call x1, Pallas kernels, local_step(): pl.pallas_call(put, out_shape=(jax.ShapeDtypeStruct((rows, d_loc), BF16),...  1.33 us

profile of v22, /device:TPU:0, one launch (start us, length us, event | category | flops | bytes accessed | tf_op | source)
XLA Modules:
  0.0 55.1 jit_solution(4670842774489479322)
XLA Ops:
  0.6 53.1 %shard_map.59 = (bf16[256,2048]{1,0:T(8,128)(2,1)S(1)}, bf16[256,2048]{1,0:T(8,128)(2,1)S(1)}) custom-call(bf16[256,2048]{1,0:T(8,128)(2,1)} %a_hbm.1, bf16[2048,8192]{1,0:T(8,128)(2,1)} %w_hbm.1, bf16[256,2048]{1,0:T(8,128)(2,1)} %r_hbm.1, f32[1,2048]{1,0:T(1,128)} %bitcast.1), custom_call_target="tpu_custom_call" | custom-call | flops 8589934592 | bytes 33554432 | tf_op jit(solution)/shard_map/pallas_call | solution.py:254
  53.7 1.3 %shard_map.60 = (bf16[256,2048]{1,0:T(8,128)(2,1)}, bf16[256,2048]{1,0:T(8,128)(2,1)}) custom-call(bf16[256,2048]{1,0:T(8,128)(2,1)S(1)} %get-tuple-element.4.hid, bf16[256,2048]{1,0:T(8,128)(2,1)S(1)} %get-tuple-element.5.nrm), custom_call_target="tpu_custom_call" | custom-call | tf_op jit(solution)/shard_map/pallas_call | solution.py:278

commit v23 on v13

--- a/solution.py
+++ b/solution.py
@@ -86,15 +86,15 @@
     def stat_copy(k, b, slot):
         return remote(st_tx.at[b], st_rx.at[slot, b], stat_tx.at[k, b], stat_rx.at[slot, b], (far, near, sib)[k])
 
+    barrier = pltpu.get_barrier_semaphore()
+    for p in (far, near, sib):
+        pl.semaphore_signal(barrier, inc=1, device_id={"tp": p}, device_id_type=MESH)
     a_copy(0).start()
     w0_copy(0).start()
     w0_copy(1).start()
     a_copy(1).start()
     r_copy = pltpu.make_async_copy(r_hbm, r_v, r_sem)
     g_copy = pltpu.make_async_copy(g_hbm, g_v, g_sem)
-    barrier = pltpu.get_barrier_semaphore()
-    for p in (far, near, sib):
-        pl.semaphore_signal(barrier, inc=1, device_id={"tp": p}, device_id_type=MESH)
 
     def dot(lhs, rhs):
         return jnp.dot(lhs, rhs, preferred_element_type=F32)
@@ -138,7 +138,7 @@
     def _(j):
         part[NEAR, :, columns(j)] = chunk(per + j, cross_col(per + j)).astype(BF16)
 
-    for b in range(n_blk):
+    for b in range(n_blk - 1):
         near_copy(b, core).start()
     r_copy.start()
     g_copy.start()
@@ -203,6 +203,10 @@
 
     for b in range(n_blk):
         reduce_block(b)
+        if b in (0, n_blk - 1):
+            @pl.when(core == (1 if b == 0 else 0))
+            def _():
+                near_copy(n_blk - 1, core).start()
 
     for b in range(n_blk):
         norm_block(b)

time: 55.1 us -> 55.2 us (level)
  no operation moved by 1% of the time
where the time goes in v23:
time: 55.2 us; the launch traced here: 55.1 us
  Pallas kernels  54.4 us (99%)
  between operations  0.64 us (1%)
    pallas_call x1, Pallas kernels, local_step(): pl.pallas_call(functools.partial(kernel, d_loc * tp), out_shape=(pltpu.VM...  53.1 us
    pallas_call x1, Pallas kernels, local_step(): pl.pallas_call(put, out_shape=(jax.ShapeDtypeStruct((rows, d_loc), BF16),...  1.33 us

profile of v23, /device:TPU:0, one launch (start us, length us, event | category | flops | bytes accessed | tf_op | source)
XLA Modules:
  0.0 55.1 jit_solution(8696810836206735635)
XLA Ops:
  0.6 53.1 %shard_map.59 = (bf16[256,2048]{1,0:T(8,128)(2,1)S(1)}, bf16[256,2048]{1,0:T(8,128)(2,1)S(1)}) custom-call(bf16[256,2048]{1,0:T(8,128)(2,1)} %a_hbm.1, bf16[2048,8192]{1,0:T(8,128)(2,1)} %w_hbm.1, bf16[256,2048]{1,0:T(8,128)(2,1)} %r_hbm.1, f32[1,2048]{1,0:T(1,128)} %bitcast.1), custom_call_target="tpu_custom_call" | custom-call | flops 8589934592 | bytes 33554432 | tf_op jit(solution)/shard_map/pallas_call | solution.py:247
  53.7 1.3 %shard_map.60 = (bf16[256,2048]{1,0:T(8,128)(2,1)}, bf16[256,2048]{1,0:T(8,128)(2,1)}) custom-call(bf16[256,2048]{1,0:T(8,128)(2,1)S(1)} %get-tuple-element.4.hid, bf16[256,2048]{1,0:T(8,128)(2,1)S(1)} %get-tuple-element.5.nrm), custom_call_target="tpu_custom_call" | custom-call | tf_op jit(solution)/shard_map/pallas_call | solution.py:271

commit v24 on v23

--- a/solution.py
+++ b/solution.py
@@ -15,6 +15,7 @@
 N_COL = 2
 BLOCKS = (128, 112, 16)
 SUB = 16
+LAG = 2
 DEPTH = 4
 PUT = 1
 FAR, NEAR, SIB = 0, 1, 2
@@ -166,50 +167,74 @@
     lane = lax.broadcasted_iota(jnp.int32, (8, 128), 1)
     sub = lax.broadcasted_iota(jnp.int32, (8, 128), 0)
 
+    edges = [sum(BLOCKS[:q]) // SUB for q in range(n_blk + 1)]
+    corr = [0, 0]
+    for q in range(2, n_blk + 1):
+        corr.append(edges[q] - edges[1] * q - sum(corr))
+
+    def first_sub(b):
+        at = b * edges[1]
+        for q in range(2, n_blk + 1):
+            at = at + jnp.minimum(b // q, 1) * corr[q]
+        return at
+
     def reduce_block(b):
-        @pl.when(core == 1)
-        def _():
-            for slot in range(2):
-                near_copy(b, slot).wait_recv()
-
-        row, n = blocks[b]
-        line = jnp.zeros((8, 128), F32)
-        for first in range(0, n, SUB):
-            sl = pl.ds(row + first, SUB)
+        for q in range(n_blk):
+            @pl.when((core == 1) & (b == q))
+            def _():
+                for slot in range(2):
+                    near_copy(q, slot).wait_recv()
+
+        base = first_sub(b)
+
+        def add(i, line):
+            row = pl.multiple_of(i * SUB, SUB)
+            sl = pl.ds(row, SUB)
             h = own[sl, :] + recv[SIB, sl, :].astype(F32) + recv[0, sl, :].astype(F32) + recv[1, sl, :].astype(F32)
             h = r_v[sl, :].astype(F32) + h
             own[sl, :] = h
             hid[sl, :] = h.astype(BF16)
             s = jnp.sum(h * h, axis=1, keepdims=True)
             for q in range(0, SUB, 8):
-                line = line + jnp.where(lane == sub + (first + q), s[q:q + 8, :], 0.0)
+                line = line + jnp.where(lane == sub + ((i - base) * SUB + q), s[q:q + 8, :], 0.0)
+            return line
+
+        line = lax.fori_loop(base, first_sub(b + 1), add, jnp.zeros((8, 128), F32))
         st_tx[b] = jnp.sum(line, axis=0, keepdims=True)
         for k in range(3):
             stat_copy(k, b, SIB if k == SIB else core).start()
 
+        @pl.when(b == (n_blk - 1) * (1 - core))
+        def _():
+            near_copy(n_blk - 1, core).start()
+
     def norm_block(b):
         for slot in range(3):
             stat_copy(slot, b, slot).wait_recv()
-        row, n = blocks[b]
+        base = first_sub(b)
         tot = (st_tx[b] + st_rx[SIB, b]) + (st_rx[0, b] + st_rx[1, b])
         scale = jnp.broadcast_to(lax.rsqrt(tot / d_model + EPS), (8, 128))
-        for first in range(0, n, SUB):
-            for q in range(first, first + SUB, 8):
-                sl = pl.ds(row + q, 8)
-                col = jnp.sum(jnp.where(lane == sub + q, scale, 0.0), axis=1, keepdims=True)
-                own[sl, :] = own[sl, :] * col * g_v[...]
-            sl = pl.ds(row + first, SUB)
-            nrm[sl, :] = own[sl, :].astype(BF16)
-
-    for b in range(n_blk):
-        reduce_block(b)
-        if b in (0, n_blk - 1):
-            @pl.when(core == (1 if b == 0 else 0))
-            def _():
-                near_copy(n_blk - 1, core).start()
-
-    for b in range(n_blk):
-        norm_block(b)
+
+        def norm(i, _):
+            row = pl.multiple_of(i * SUB, SUB)
+            out = []
+            for q in range(0, SUB, 8):
+                col = jnp.sum(jnp.where(lane == sub + ((i - base) * SUB + q), scale, 0.0), axis=1, keepdims=True)
+                out.append(own[pl.ds(pl.multiple_of(row + q, 8), 8), :] * col * g_v[...])
+            nrm[pl.ds(row, SUB), :] = jnp.concatenate(out, axis=0).astype(BF16)
+            return 0
+
+        lax.fori_loop(base, first_sub(b + 1), norm, 0)
+
+    @pl.loop(0, n_blk + LAG)
+    def _(b):
+        @pl.when(b < n_blk)
+        def _():
+            reduce_block(b)
+
+        @pl.when(b >= LAG)
+        def _():
+            norm_block(b - LAG)
 
     for q in range(len(far_parts)):
         far_copy(q, core).wait_send()

time: 55.2 us -> 55.7 us (level)
  Pallas kernels: 54.4 us -> 55 us
where the time goes in v24:
time: 55.7 us; the launch traced here: 55.6 us
  Pallas kernels  55 us (99%)
  between operations  0.64 us (1%)
    pallas_call x1, Pallas kernels, local_step(): pl.pallas_call(functools.partial(kernel, d_loc * tp), out_shape=(pltpu.VM...  53.6 us
    pallas_call x1, Pallas kernels, local_step(): pl.pallas_call(put, out_shape=(jax.ShapeDtypeStruct((rows, d_loc), BF16),...  1.33 us

profile of v24, /device:TPU:0, one launch (start us, length us, event | category | flops | bytes accessed | tf_op | source)
XLA Modules:
  0.0 55.6 jit_solution(4091186937424044837)
XLA Ops:
  0.6 53.6 %shard_map.59 = (bf16[256,2048]{1,0:T(8,128)(2,1)S(1)}, bf16[256,2048]{1,0:T(8,128)(2,1)S(1)}) custom-call(bf16[256,2048]{1,0:T(8,128)(2,1)} %a_hbm.1, bf16[2048,8192]{1,0:T(8,128)(2,1)} %w_hbm.1, bf16[256,2048]{1,0:T(8,128)(2,1)} %r_hbm.1, f32[1,2048]{1,0:T(1,128)} %bitcast.1), custom_call_target="tpu_custom_call" | custom-call | flops 8589934592 | bytes 33554432 | tf_op jit(solution)/shard_map/pallas_call | solution.py:272
  54.3 1.3 %shard_map.60 = (bf16[256,2048]{1,0:T(8,128)(2,1)}, bf16[256,2048]{1,0:T(8,128)(2,1)}) custom-call(bf16[256,2048]{1,0:T(8,128)(2,1)S(1)} %get-tuple-element.4.hid, bf16[256,2048]{1,0:T(8,128)(2,1)S(1)} %get-tuple-element.5.nrm), custom_call_target="tpu_custom_call" | custom-call | tf_op jit(solution)/shard_map/pallas_call | solution.py:296

commit v25 on v18

--- a/solution.py
+++ b/solution.py
@@ -69,8 +69,8 @@
                                             device_id={"tp": peer}, device_id_type=MESH)
 
     every = pl.ds(0, rows)
-    far_parts = [(pl.ds(0, half), pl.ds(0, lanes)), (pl.ds(0, half), pl.ds(lanes, lanes)), (pl.ds(half, half), pl.ds(0, CW))]
-    far_parts += [(every, pl.ds(j * CW, CW)) for j in range(1, N_COL)]
+    pieces = ((pl.ds(0, half), pl.ds(0, lanes)), (pl.ds(0, half), pl.ds(lanes, lanes)), (pl.ds(half, half), pl.ds(0, CW)))
+    far_parts = [(every, pl.ds(j * CW, CW)) for j in range(N_COL)]
     far_parts += [(every, pl.ds(N_COL * CW, d_loc - N_COL * CW))]
 
     def far_copy(q, slot):
@@ -113,11 +113,11 @@
         else:
             a_copy(1).wait()
             w_start(DEPTH)
-        r_sl, c_sl = far_parts[q]
+        r_sl, c_sl = pieces[q]
         part[FAR, r_sl, c_sl] = dot(a_v[r_sl, :], w_v[0, :, c_sl]).astype(BF16)
-        if q == 0:
-            pl.semaphore_wait(barrier, 3)
-        far_copy(q, core).start()
+
+    pl.semaphore_wait(barrier, 3)
+    far_copy(0, core).start()
 
     def chunk(i, col):
         w_copy(i, col).wait()
@@ -129,7 +129,7 @@
 
     for j in range(1, N_COL):
         part[FAR, :, columns(j)] = chunk(j, cross_col(j)).astype(BF16)
-        far_copy(2 + j, core).start()
+        far_copy(j, core).start()
 
     @pl.loop(N_COL, per)
     def _(j):
@@ -261,7 +261,7 @@
                 pltpu.VMEM((n_blk, 1, 128), F32),
                 pltpu.VMEM((3, n_blk, 1, 128), F32),
                 dma((2,)), dma((2,)), dma((4 * per,)), dma, dma,
-                dma((N_COL + 3,)), dma((2, N_COL + 3)), dma((len(NEAR_ROWS),)), dma((2, len(NEAR_ROWS))), dma, dma,
+                dma((N_COL + 1,)), dma((2, N_COL + 1)), dma((len(NEAR_ROWS),)), dma((2, len(NEAR_ROWS))), dma, dma,
                 dma((3, n_blk)), dma((3, n_blk)),
             ],
             compiler_params=pltpu.CompilerParams(

time: 55.1 us -> 55 us (level)
  no operation moved by 1% of the time
where the time goes in v25:
time: 55 us; the launch traced here: 54.9 us
  Pallas kernels  54.3 us (99%)
  between operations  0.64 us (1%)
    pallas_call x1, Pallas kernels, local_step(): pl.pallas_call(functools.partial(kernel, d_loc * tp), out_shape=(pltpu.VM...  52.9 us
    pallas_call x1, Pallas kernels, local_step(): pl.pallas_call(put, out_shape=(jax.ShapeDtypeStruct((rows, d_loc), BF16),...  1.33 us

profile of v25, /device:TPU:0, one launch (start us, length us, event | category | flops | bytes accessed | tf_op | source)
XLA Modules:
  0.0 54.9 jit_solution(10537986535653658413)
XLA Ops:
  0.6 52.9 %shard_map.59 = (bf16[256,2048]{1,0:T(8,128)(2,1)S(1)}, bf16[256,2048]{1,0:T(8,128)(2,1)S(1)}) custom-call(bf16[256,2048]{1,0:T(8,128)(2,1)} %a_hbm.1, bf16[2048,8192]{1,0:T(8,128)(2,1)} %w_hbm.1, bf16[256,2048]{1,0:T(8,128)(2,1)} %r_hbm.1, f32[1,2048]{1,0:T(1,128)} %bitcast.1), custom_call_target="tpu_custom_call" | custom-call | flops 8589934592 | bytes 33554432 | tf_op jit(solution)/shard_map/pallas_call | solution.py:248
  53.6 1.3 %shard_map.60 = (bf16[256,2048]{1,0:T(8,128)(2,1)}, bf16[256,2048]{1,0:T(8,128)(2,1)}) custom-call(bf16[256,2048]{1,0:T(8,128)(2,1)S(1)} %get-tuple-element.4.hid, bf16[256,2048]{1,0:T(8,128)(2,1)S(1)} %get-tuple-element.5.nrm), custom_call_target="tpu_custom_call" | custom-call | tf_op jit(solution)/shard_map/pallas_call | solution.py:272

commit v26 on v25

--- a/solution.py
+++ b/solution.py
@@ -13,8 +13,8 @@
 
 CW = 256
 N_COL = 2
-BLOCKS = (128, 112, 16)
-NEAR_ROWS = (240, 16)
+BLOCKS = (128, 64, 48, 16)
+NEAR_ROWS = (192, 48, 16)
 SUB = 16
 DEPTH = 4
 PUT = 1

time: 55 us -> 55.1 us (level)
  no operation moved by 1% of the time
where the time goes in v26:
time: 55.1 us; the launch traced here: 55 us
  Pallas kernels  54.4 us (99%)
  between operations  0.64 us (1%)
    pallas_call x1, Pallas kernels, local_step(): pl.pallas_call(functools.partial(kernel, d_loc * tp), out_shape=(pltpu.VM...  53 us
    pallas_call x1, Pallas kernels, local_step(): pl.pallas_call(put, out_shape=(jax.ShapeDtypeStruct((rows, d_loc), BF16),...  1.33 us

profile of v26, /device:TPU:0, one launch (start us, length us, event | category | flops | bytes accessed | tf_op | source)
XLA Modules:
  0.0 55.0 jit_solution(126936040526950035)
XLA Ops:
  0.6 53.0 %shard_map.59 = (bf16[256,2048]{1,0:T(8,128)(2,1)S(1)}, bf16[256,2048]{1,0:T(8,128)(2,1)S(1)}) custom-call(bf16[256,2048]{1,0:T(8,128)(2,1)} %a_hbm.1, bf16[2048,8192]{1,0:T(8,128)(2,1)} %w_hbm.1, bf16[256,2048]{1,0:T(8,128)(2,1)} %r_hbm.1, f32[1,2048]{1,0:T(1,128)} %bitcast.1), custom_call_target="tpu_custom_call" | custom-call | flops 8589934592 | bytes 33554432 | tf_op jit(solution)/shard_map/pallas_call | solution.py:248
  53.7 1.3 %shard_map.60 = (bf16[256,2048]{1,0:T(8,128)(2,1)}, bf16[256,2048]{1,0:T(8,128)(2,1)}) custom-call(bf16[256,2048]{1,0:T(8,128)(2,1)S(1)} %get-tuple-element.4.hid, bf16[256,2048]{1,0:T(8,128)(2,1)S(1)} %get-tuple-element.5.nrm), custom_call_target="tpu_custom_call" | custom-call | tf_op jit(solution)/shard_map/pallas_call | solution.py:272

commit v27 on v26

--- a/solution.py
+++ b/solution.py
@@ -13,8 +13,8 @@
 
 CW = 256
 N_COL = 2
-BLOCKS = (128, 64, 48, 16)
-NEAR_ROWS = (192, 48, 16)
+BLOCKS = (128, 96, 32)
+NEAR_ROWS = (224, 32)
 SUB = 16
 DEPTH = 4
 PUT = 1

time: 55.1 us -> 55 us (level)
  no operation moved by 1% of the time
where the time goes in v27:
time: 55 us; the launch traced here: 54.9 us
  Pallas kernels  54.3 us (99%)
  between operations  0.64 us (1%)
    pallas_call x1, Pallas kernels, local_step(): pl.pallas_call(functools.partial(kernel, d_loc * tp), out_shape=(pltpu.VM...  53 us
    pallas_call x1, Pallas kernels, local_step(): pl.pallas_call(put, out_shape=(jax.ShapeDtypeStruct((rows, d_loc), BF16),...  1.33 us

profile of v27, /device:TPU:0, one launch (start us, length us, event | category | flops | bytes accessed | tf_op | source)
XLA Modules:
  0.0 54.9 jit_solution(13069821467005078740)
XLA Ops:
  0.6 53.0 %shard_map.59 = (bf16[256,2048]{1,0:T(8,128)(2,1)S(1)}, bf16[256,2048]{1,0:T(8,128)(2,1)S(1)}) custom-call(bf16[256,2048]{1,0:T(8,128)(2,1)} %a_hbm.1, bf16[2048,8192]{1,0:T(8,128)(2,1)} %w_hbm.1, bf16[256,2048]{1,0:T(8,128)(2,1)} %r_hbm.1, f32[1,2048]{1,0:T(1,128)} %bitcast.1), custom_call_target="tpu_custom_call" | custom-call | flops 8589934592 | bytes 33554432 | tf_op jit(solution)/shard_map/pallas_call | solution.py:248
  53.6 1.3 %shard_map.60 = (bf16[256,2048]{1,0:T(8,128)(2,1)}, bf16[256,2048]{1,0:T(8,128)(2,1)}) custom-call(bf16[256,2048]{1,0:T(8,128)(2,1)S(1)} %get-tuple-element.4.hid, bf16[256,2048]{1,0:T(8,128)(2,1)S(1)} %get-tuple-element.5.nrm), custom_call_target="tpu_custom_call" | custom-call | tf_op jit(solution)/shard_map/pallas_call | solution.py:272

commit v28 on v25

--- a/solution.py
+++ b/solution.py
@@ -160,6 +160,11 @@
     g_copy.wait()
     sib_copy().wait_recv()
 
+    @pl.loop(0, rows // SUB)
+    def _(i):
+        sl = pl.ds(pl.multiple_of(i * SUB, SUB), SUB)
+        own[sl, :] = (own[sl, :] + recv[SIB, sl, :].astype(F32)) + r_v[sl, :].astype(F32)
+
     @pl.when(core == 0)
     def _():
         for q in range(len(far_parts)):
@@ -180,8 +185,7 @@
         line = jnp.zeros((8, 128), F32)
         for first in range(0, n, SUB):
             sl = pl.ds(row + first, SUB)
-            h = own[sl, :] + recv[SIB, sl, :].astype(F32) + recv[0, sl, :].astype(F32) + recv[1, sl, :].astype(F32)
-            h = r_v[sl, :].astype(F32) + h
+            h = own[sl, :] + (recv[0, sl, :].astype(F32) + recv[1, sl, :].astype(F32))
             own[sl, :] = h
             hid[sl, :] = h.astype(BF16)
             s = jnp.sum(h * h, axis=1, keepdims=True)

time: 55 us -> 55 us (level)
  no operation moved by 1% of the time
where the time goes in v28:
time: 55 us; the launch traced here: 54.9 us
  Pallas kernels  54.2 us (99%)
  between operations  0.64 us (1%)
    pallas_call x1, Pallas kernels, local_step(): pl.pallas_call(functools.partial(kernel, d_loc * tp), out_shape=(pltpu.VM...  52.9 us
    pallas_call x1, Pallas kernels, local_step(): pl.pallas_call(put, out_shape=(jax.ShapeDtypeStruct((rows, d_loc), BF16),...  1.33 us

profile of v28, /device:TPU:0, one launch (start us, length us, event | category | flops | bytes accessed | tf_op | source)
XLA Modules:
  0.0 54.9 jit_solution(17202418002930719566)
XLA Ops:
  0.6 52.9 %shard_map.59 = (bf16[256,2048]{1,0:T(8,128)(2,1)S(1)}, bf16[256,2048]{1,0:T(8,128)(2,1)S(1)}) custom-call(bf16[256,2048]{1,0:T(8,128)(2,1)} %a_hbm.1, bf16[2048,8192]{1,0:T(8,128)(2,1)} %w_hbm.1, bf16[256,2048]{1,0:T(8,128)(2,1)} %r_hbm.1, f32[1,2048]{1,0:T(1,128)} %bitcast.1), custom_call_target="tpu_custom_call" | custom-call | flops 8589934592 | bytes 33554432 | tf_op jit(solution)/shard_map/pallas_call | solution.py:252
  53.5 1.3 %shard_map.60 = (bf16[256,2048]{1,0:T(8,128)(2,1)}, bf16[256,2048]{1,0:T(8,128)(2,1)}) custom-call(bf16[256,2048]{1,0:T(8,128)(2,1)S(1)} %get-tuple-element.4.hid, bf16[256,2048]{1,0:T(8,128)(2,1)S(1)} %get-tuple-element.5.nrm), custom_call_target="tpu_custom_call" | custom-call | tf_op jit(solution)/shard_map/pallas_call | solution.py:276

commit v29 on v28

--- a/solution.py
+++ b/solution.py
@@ -202,12 +202,11 @@
         tot = (st_tx[b] + st_rx[SIB, b]) + (st_rx[0, b] + st_rx[1, b])
         scale = jnp.broadcast_to(lax.rsqrt(tot / d_model + EPS), (8, 128))
         for first in range(0, n, SUB):
+            out = []
             for q in range(first, first + SUB, 8):
-                sl = pl.ds(row + q, 8)
                 col = jnp.sum(jnp.where(lane == sub + q, scale, 0.0), axis=1, keepdims=True)
-                own[sl, :] = own[sl, :] * col * g_v[...]
-            sl = pl.ds(row + first, SUB)
-            nrm[sl, :] = own[sl, :].astype(BF16)
+                out.append(own[pl.ds(row + q, 8), :] * col * g_v[...])
+            nrm[pl.ds(row + first, SUB), :] = jnp.concatenate(out, axis=0).astype(BF16)
 
     for b in range(n_blk):
         reduce_block(b)

time: 55 us -> 55 us (level)
  no operation moved by 1% of the time
where the time goes in v29:
time: 55 us; the launch traced here: 54.9 us
  Pallas kernels  54.2 us (99%)
  between operations  0.64 us (1%)
    pallas_call x1, Pallas kernels, local_step(): pl.pallas_call(functools.partial(kernel, d_loc * tp), out_shape=(pltpu.VM...  52.9 us
    pallas_call x1, Pallas kernels, local_step(): pl.pallas_call(put, out_shape=(jax.ShapeDtypeStruct((rows, d_loc), BF16),...  1.33 us

profile of v29, /device:TPU:0, one launch (start us, length us, event | category | flops | bytes accessed | tf_op | source)
XLA Modules:
  0.0 54.9 jit_solution(4859655722230360563)
XLA Ops:
  0.6 52.9 %shard_map.59 = (bf16[256,2048]{1,0:T(8,128)(2,1)S(1)}, bf16[256,2048]{1,0:T(8,128)(2,1)S(1)}) custom-call(bf16[256,2048]{1,0:T(8,128)(2,1)} %a_hbm.1, bf16[2048,8192]{1,0:T(8,128)(2,1)} %w_hbm.1, bf16[256,2048]{1,0:T(8,128)(2,1)} %r_hbm.1, f32[1,2048]{1,0:T(1,128)} %bitcast.1), custom_call_target="tpu_custom_call" | custom-call | flops 8589934592 | bytes 33554432 | tf_op jit(solution)/shard_map/pallas_call | solution.py:251
  53.5 1.3 %shard_map.60 = (bf16[256,2048]{1,0:T(8,128)(2,1)}, bf16[256,2048]{1,0:T(8,128)(2,1)}) custom-call(bf16[256,2048]{1,0:T(8,128)(2,1)S(1)} %get-tuple-element.4.hid, bf16[256,2048]{1,0:T(8,128)(2,1)S(1)} %get-tuple-element.5.nrm), custom_call_target="tpu_custom_call" | custom-call | tf_op jit(solution)/shard_map/pallas_call | solution.py:275

commit v30 on v29

--- a/solution.py
+++ b/solution.py
@@ -70,7 +70,7 @@
 
     every = pl.ds(0, rows)
     pieces = ((pl.ds(0, half), pl.ds(0, lanes)), (pl.ds(0, half), pl.ds(lanes, lanes)), (pl.ds(half, half), pl.ds(0, CW)))
-    far_parts = [(every, pl.ds(j * CW, CW)) for j in range(N_COL)]
+    far_parts = [(every, pl.ds(0, N_COL * CW))]
     far_parts += [(every, pl.ds(N_COL * CW, d_loc - N_COL * CW))]
 
     def far_copy(q, slot):
@@ -116,8 +116,6 @@
         r_sl, c_sl = pieces[q]
         part[FAR, r_sl, c_sl] = dot(a_v[r_sl, :], w_v[0, :, c_sl]).astype(BF16)
 
-    pl.semaphore_wait(barrier, 3)
-    far_copy(0, core).start()
 
     def chunk(i, col):
         w_copy(i, col).wait()
@@ -129,7 +127,9 @@
 
     for j in range(1, N_COL):
         part[FAR, :, columns(j)] = chunk(j, cross_col(j)).astype(BF16)
-        far_copy(j, core).start()
+
+    pl.semaphore_wait(barrier, 3)
+    far_copy(0, core).start()
 
     @pl.loop(N_COL, per)
     def _(j):
@@ -264,7 +264,7 @@
                 pltpu.VMEM((n_blk, 1, 128), F32),
                 pltpu.VMEM((3, n_blk, 1, 128), F32),
                 dma((2,)), dma((2,)), dma((4 * per,)), dma, dma,
-                dma((N_COL + 1,)), dma((2, N_COL + 1)), dma((len(NEAR_ROWS),)), dma((2, len(NEAR_ROWS))), dma, dma,
+                dma((2,)), dma((2, 2)), dma((len(NEAR_ROWS),)), dma((2, len(NEAR_ROWS))), dma, dma,
                 dma((3, n_blk)), dma((3, n_blk)),
             ],
             compiler_params=pltpu.CompilerParams(

time: 55 us -> 55.6 us (1.011)
  Pallas kernels: 54.2 us -> 54.8 us
    pallas_call x1, Pallas kernels: 52.9 us -> 53.5 us  [local_step(): pl.pallas_call(functools.partial(kernel, d_loc * tp), out_shape=(pltpu.VM...]
where the time goes in v30:
time: 55.6 us; the launch traced here: 55.4 us
  Pallas kernels  54.8 us (99%)
  between operations  0.64 us (1%)
    pallas_call x1, Pallas kernels, local_step(): pl.pallas_call(functools.partial(kernel, d_loc * tp), out_shape=(pltpu.VM...  53.5 us
    pallas_call x1, Pallas kernels, local_step(): pl.pallas_call(put, out_shape=(jax.ShapeDtypeStruct((rows, d_loc), BF16),...  1.33 us

profile of v30, /device:TPU:0, one launch (start us, length us, event | category | flops | bytes accessed | tf_op | source)
XLA Modules:
  0.0 55.4 jit_solution(4047726424240630719)
XLA Ops:
  0.6 53.5 %shard_map.59 = (bf16[256,2048]{1,0:T(8,128)(2,1)S(1)}, bf16[256,2048]{1,0:T(8,128)(2,1)S(1)}) custom-call(bf16[256,2048]{1,0:T(8,128)(2,1)} %a_hbm.1, bf16[2048,8192]{1,0:T(8,128)(2,1)} %w_hbm.1, bf16[256,2048]{1,0:T(8,128)(2,1)} %r_hbm.1, f32[1,2048]{1,0:T(1,128)} %bitcast.1), custom_call_target="tpu_custom_call" | custom-call | flops 8589934592 | bytes 33554432 | tf_op jit(solution)/shard_map/pallas_call | solution.py:251
  54.1 1.3 %shard_map.60 = (bf16[256,2048]{1,0:T(8,128)(2,1)}, bf16[256,2048]{1,0:T(8,128)(2,1)}) custom-call(bf16[256,2048]{1,0:T(8,128)(2,1)S(1)} %get-tuple-element.4.hid, bf16[256,2048]{1,0:T(8,128)(2,1)S(1)} %get-tuple-element.5.nrm), custom_call_target="tpu_custom_call" | custom-call | tf_op jit(solution)/shard_map/pallas_call | solution.py:275
